TPU v7x, 32 devices: a whole 2x2x4 slice. The times are simulated.
32 devices in a mesh: layout: 2 (over x), tile: 8 (over z, y), chan: 2 (over core).
Axes of the slice: x: 2, y: 2, z: 4, core: 2. Of those that a mesh axis runs over, the one named last changes fastest.
Arguments:
- sample_weight: float32 [32, 64, 256], P(('layout', 'tile', 'chan')), parts along dimension 0, may hold values from 0.25 to 4
- fraction_u: float32 [32, 64, 256], P(('layout', 'tile', 'chan')), parts along dimension 0, may hold values from 0 to 1
- fraction_v: float32 [32, 64, 256], P(('layout', 'tile', 'chan')), parts along dimension 0, may hold values from 0 to 1
- cell_code: int32 [32, 64, 256], P(('layout', 'tile', 'chan')), parts along dimension 0, may hold values from 260 to 3835, as said below
- tile_fill: int32 [32, 64, 64], P(('layout', 'tile', 'chan')), parts along dimension 0, may hold values from 0 to 4, as said below
Outputs:
- psf: float32 [8192, 4096], P(('layout', 'tile', 'chan')), parts along dimension 0
There are 2 independent parts, one for each index of `layout`. A program takes and returns all parts, laid end to end along the dimension named above; each array names one. Nothing has to cross between parts.
Inputs may be any that keep to these rules, and one draw needn't show every extreme that they name: `cell_code`: row offset and column offset each lie in 4 .. 59. `tile_fill`: some uv tile is full from every sender; tiles near the grid's centre hold more samples than outer ones.
All inputs are finite; a program needn't handle non-finite values.
Results may differ from a plain program's by a relative error of at most 0.0003.
Values sent between devices are 32-bit elements; how exact they have to be, the bound alone decides.
No kernel may reach another device: no remote copies, remote signals or barrier semaphores. Data moves between devices by JAX's collectives and lax.ppermute only.
A program may use at most 64 MiB of HBM per device.

v0:
```python
import math

import jax
import jax.numpy as jnp
import numpy as np
from jax import lax
from jax.experimental import pallas as pl
from jax.experimental.pallas import tpu as pltpu
from jax.sharding import Mesh, PartitionSpec as P

G = 4096
TILE = 64
HALF = 3
CAP = 4
NT = 64


HIGHEST = lax.Precision.HIGHEST


def taper(distance):
    scaled = distance / (HALF + 1.0)
    inner = 1.0 - scaled * scaled
    return jnp.where(inner > 0.0, inner * inner, 0.0 * inner)


def angles(left_count, right_count, period):
    product = (
        jnp.arange(left_count, dtype=jnp.int32)[:, None]
        * jnp.arange(right_count, dtype=jnp.int32)[None, :]
    )
    phase = (product % period).astype(jnp.float32) * (2.0 * math.pi / period)
    return (jnp.cos(phase), jnp.sin(phase))


def grid_row(weight_row, frac_row_u, frac_row_v, code_row, fill_row):
    sources = weight_row.shape[0]
    cell_pos = jnp.arange(TILE).astype(jnp.float32)
    slot_index = jnp.arange(CAP, dtype=jnp.int32)
    weight_row = weight_row.reshape(sources, NT, CAP)
    code_row = code_row.reshape(sources, NT, CAP)
    is_live = slot_index[None, None, :] < fill_row[:, :, None]
    live_weight = jnp.where(is_live, weight_row, 0.0)
    row_off = (code_row // TILE).astype(jnp.float32) + frac_row_u.reshape(sources, NT, CAP)
    col_off = (code_row % TILE).astype(jnp.float32) + frac_row_v.reshape(sources, NT, CAP)
    kernel_u = taper(cell_pos - row_off[..., None]) * live_weight[..., None]
    kernel_v = taper(cell_pos - col_off[..., None])
    tiles = jnp.einsum("sncu,sncv->unv", kernel_u, kernel_v, precision=HIGHEST)
    return tiles.reshape(TILE, G)


def row_pass(slab):
    slab_rows = slab.shape[0]
    blocks = slab.reshape(slab_rows, NT, TILE)
    cos_small, sin_small = angles(NT, NT, NT)
    first_re = jnp.einsum("rab,ak->rkb", blocks, cos_small, precision=HIGHEST)
    first_im = jnp.einsum("rab,ak->rkb", blocks, sin_small, precision=HIGHEST)
    cos_twist, sin_twist = angles(NT, TILE, G)
    turned_re = first_re * cos_twist - first_im * sin_twist
    turned_im = first_re * sin_twist + first_im * cos_twist
    cos_large, sin_large = angles(TILE, TILE, TILE)
    out_re = jnp.einsum("rkb,bj->rjk", turned_re, cos_large, precision=HIGHEST) - jnp.einsum(
        "rkb,bj->rjk", turned_im, sin_large, precision=HIGHEST
    )
    out_im = jnp.einsum("rkb,bj->rjk", turned_re, sin_large, precision=HIGHEST) + jnp.einsum(
        "rkb,bj->rjk", turned_im, cos_large, precision=HIGHEST
    )
    return (out_re.reshape(slab_rows, G), out_im.reshape(slab_rows, G))


def column_pass(part_re, part_im):
    col_count = part_re.shape[1]
    blocks_re = part_re.reshape(NT, TILE, col_count)
    blocks_im = part_im.reshape(NT, TILE, col_count)
    cos_small, sin_small = angles(NT, NT, NT)
    first_re = jnp.einsum("abc,ak->kbc", blocks_re, cos_small, precision=HIGHEST) - jnp.einsum(
        "abc,ak->kbc", blocks_im, sin_small, precision=HIGHEST
    )
    first_im = jnp.einsum("abc,ak->kbc", blocks_re, sin_small, precision=HIGHEST) + jnp.einsum(
        "abc,ak->kbc", blocks_im, cos_small, precision=HIGHEST
    )
    cos_twist, sin_twist = angles(NT, TILE, G)
    turned_re = first_re * cos_twist[:, :, None] - first_im * sin_twist[:, :, None]
    turned_im = first_re * sin_twist[:, :, None] + first_im * cos_twist[:, :, None]
    cos_large, sin_large = angles(TILE, TILE, TILE)
    real_part = jnp.einsum("kbc,bj->cjk", turned_re, cos_large, precision=HIGHEST) - jnp.einsum(
        "kbc,bj->cjk", turned_im, sin_large, precision=HIGHEST
    )
    return real_part.reshape(col_count, G)


def general_body(sample_weight, fraction_u, fraction_v, cell_code, tile_fill):
    landed_weight, landed_frac_u, landed_frac_v = (
        lax.all_to_all(sample_weight, "tile", split_axis=1, concat_axis=0, tiled=True),
        lax.all_to_all(fraction_u, "tile", split_axis=1, concat_axis=0, tiled=True),
        lax.all_to_all(fraction_v, "tile", split_axis=1, concat_axis=0, tiled=True),
    )
    landed_code, landed_fill = (
        lax.all_to_all(cell_code, "tile", split_axis=1, concat_axis=0, tiled=True),
        lax.all_to_all(tile_fill, "tile", split_axis=1, concat_axis=0, tiled=True),
    )
    own_rows = landed_weight.shape[1]
    row_slabs = []
    for local_row in range(own_rows):
        row_slabs.append(
            grid_row(
                landed_weight[:, local_row],
                landed_frac_u[:, local_row],
                landed_frac_v[:, local_row],
                landed_code[:, local_row],
                landed_fill[:, local_row],
            )
        )
    slab = jnp.concatenate(row_slabs, axis=0)
    tile_count = lax.axis_size("tile")
    chan_count = lax.axis_size("chan")
    shared = lax.psum_scatter(slab, "chan", scatter_dimension=0, tiled=True)
    spectrum_re, spectrum_im = row_pass(shared)
    column_re, column_im = (
        lax.all_to_all(spectrum_re, ("tile", "chan"), split_axis=1, concat_axis=0, tiled=True),
        lax.all_to_all(spectrum_im, ("tile", "chan"), split_axis=1, concat_axis=0, tiled=True),
    )
    norm_scale = 1.0 / math.sqrt(tile_count * chan_count * NT * NT * CAP)
    return column_pass(column_re, column_im) * norm_scale


HALVES = 2
LANES = 2 * TILE
COARSE = G // LANES
SLABS = NT // 4
HERM = COARSE // 2 + 1
STEP = COARSE + 1
STRIP = 16
LAST = SLABS // 4 - 1
BF16 = jnp.bfloat16
F32 = jnp.float32


def split(value):
    high = value.astype(BF16)
    return high, (value - high.astype(F32)).astype(BF16)


def split_constant(value):
    high = value.astype(np.float32).astype(BF16)
    low = (value - high.astype(np.float64)).astype(np.float32).astype(BF16)
    return high, low


def exact_pieces(value):
    high, rest = value.astype(BF16), None
    rest = value - high.astype(F32)
    middle = rest.astype(BF16)
    return high, middle, (rest - middle.astype(F32)).astype(BF16)


def times(value, turn):
    real, imag = value
    turn = turn % 1.0
    if turn == 0.0 or (real is None and imag is None):
        return value
    if turn == 0.25:
        return (None if imag is None else -imag, real)
    if turn == 0.5:
        return (-real, None if imag is None else -imag)
    c, s = math.cos(2 * math.pi * turn), math.sin(2 * math.pi * turn)
    if imag is None:
        return (real * c, real * s)
    if turn == 0.125:
        return ((real - imag) * c, (real + imag) * c)
    if turn == 0.375:
        return ((real + imag) * c, (real - imag) * s)
    return (real * c - imag * s, real * s + imag * c)


def plus(x, y):
    if x is None:
        return y
    return x if y is None else x + y


def minus(x, y):
    if y is None:
        return x
    return -y if x is None else x - y


def real_transform(values):
    n = len(values)
    if n == 1:
        return [(values[0], None)]
    if n == 2:
        return [(values[0] + values[1], None), (values[0] - values[1], None)]
    even, odd = real_transform(values[0::2]), real_transform(values[1::2])
    out = [None] * (n // 2 + 1)
    for k in range(n // 4 + 1):
        e, t = even[k], times(odd[k], k / n)
        out[k] = (plus(e[0], t[0]), plus(e[1], t[1]))
        if n // 2 - k != k:
            out[n // 2 - k] = (minus(e[0], t[0]), minus(t[1], e[1]))
    return out


def complex_transform(values):
    n = len(values)
    if n == 1:
        return values
    even, odd = complex_transform(values[0::2]), complex_transform(values[1::2])
    out = [None] * n
    for k in range(n // 2):
        e, t = even[k], times(odd[k], k / n)
        out[k] = (plus(e[0], t[0]), plus(e[1], t[1]))
        out[k + n // 2] = (minus(e[0], t[0]), minus(e[1], t[1]))
    return out


def pack_kernel(weight_ref, frac_u_ref, frac_v_ref, code_ref, fill_ref, *rest):
    phases = len(rest) - 7
    out_refs, (real_ref, whole_ref, used_ref, stage_ref, rows_ref, done, landed) = rest[:phases], rest[phases:]
    loads = [
        pltpu.make_async_copy(source, target, landed.at[i])
        for i, (source, target) in enumerate(
            (
                (fill_ref, used_ref),
                (weight_ref, real_ref.at[0:1]),
                (code_ref, whole_ref),
                (frac_u_ref, real_ref.at[1:2]),
                (frac_v_ref, real_ref.at[2:3]),
            )
        )
    ]
    for load in loads:
        load.start()
    wide = NT * CAP
    row = lax.broadcasted_iota(jnp.int32, (NT, wide), 0)
    lane = lax.broadcasted_iota(jnp.int32, (NT, wide), 1)
    spread = jnp.where(lane // CAP == row, 1.0, 0.0).astype(BF16)
    kappa = lax.broadcasted_iota(jnp.int32, (2 * wide, CAP * LANES), 0)
    target = lax.broadcasted_iota(jnp.int32, (2 * wide, CAP * LANES), 1)
    parity, column, slot = kappa // wide, (kappa % wide) // CAP, kappa % CAP
    place = parity * NT + column
    low = jnp.where(target == slot * LANES + place, 1.0, 0.0).astype(BF16)
    high = jnp.where(target == slot * LANES + (LANES - 1 - place), 1.0, 0.0).astype(BF16)
    for load in loads:
        load.wait()
    filled = jnp.dot(used_ref[0].astype(F32).astype(BF16), spread, preferred_element_type=F32)
    live = jnp.where((lane % CAP).astype(F32) < filled, real_ref[0], 0.0)
    code = whole_ref[0]
    place_u = (code // TILE).astype(F32) + real_ref[1]
    place_v = (code % TILE).astype(F32) + real_ref[2]
    folded = row >= NT // 2
    place_u = jnp.where(folded, TILE - place_u, place_u)
    place_v = jnp.where(folded, TILE - place_v, place_v)
    for arr, value in enumerate((live, place_u, place_v)):
        for part in range(2):
            stage_ref[2 * arr + part] = value[:, part * LANES : (part + 1) * LANES]
    pairs = NT // 2
    rows = [
        jnp.concatenate(
            [stage_ref[2 * arr + part, pl.ds(parity, pairs, stride=2), :] for parity in range(2) for part in range(2)],
            axis=1,
        )
        for arr in range(3)
    ]
    for fold, permute in enumerate((low, high)):
        chosen = jnp.concatenate([value[fold * SLABS : (fold + 1) * SLABS] for value in rows], axis=0)
        moved = sum(jnp.dot(piece, permute, preferred_element_type=F32) for piece in exact_pieces(chosen))
        for arr in range(3):
            for slot in range(CAP):
                block = moved[arr * SLABS : (arr + 1) * SLABS, slot * LANES : (slot + 1) * LANES]
                at = arr * 2 * CAP + fold * CAP + slot
                for slab in range(SLABS):
                    chosen_row = SLABS - 1 - slab if fold else slab
                    rows_ref[slab, pl.ds(at, 1), :] = block[chosen_row : chosen_row + 1]
    copies = []
    for phase, out_ref in enumerate(out_refs):
        devices, steps = out_ref.shape[0], out_ref.shape[1]
        for device in range(devices):
            first = owned(device // 2 % 4, device % 2) + phase * steps
            copies.append(
                pltpu.make_async_copy(rows_ref.at[pl.ds(first, steps)], out_ref.at[device], done.at[len(copies)])
            )
            copies[-1].start()
    for copy in copies:
        copy.wait()


def owned(chip, core):
    return SLABS // 2 * ((chip // 2) ^ (chip % 2)) + SLABS // 4 * core


def grid_kernel(k, local, taps_ref, matrix_from, twist_from, *rest):
    *refs, place_ref, grid_ref, high_ref, low_ref, matrix_ref, twist_ref, landed = rest
    out_refs = [refs[-4].at[k], *refs[-3:]]
    loads = [
        pltpu.make_async_copy(twist_from, twist_ref, landed.at[0]),
        pltpu.make_async_copy(matrix_from, matrix_ref, landed.at[1]),
    ]
    for load in loads:
        load.start()
    count = 2 * CAP * taps_ref.shape[0]
    for arr in range(3):
        value = taps_ref[:, local, arr * 2 * CAP : (arr + 1) * 2 * CAP, :].reshape(count, LANES)
        place_ref[arr] = value.T
    cell = lax.broadcasted_iota(jnp.int32, (TILE, count), 0).astype(F32)
    support = (HALF + 1.0) * (HALF + 1.0)

    def bump(offset):
        inner = jnp.maximum(support - offset * offset, 0.0)
        return inner * inner

    def column(j, carry):
        sums = []
        for row in range(2):
            at = row * NT + j
            tap_u = bump(cell - place_ref[1, pl.ds(at, 1), :])
            tap_v = bump(cell - place_ref[2, pl.ds(at, 1), :]) * place_ref[0, pl.ds(at, 1), :]
            u_high, u_low = split(tap_u)
            v_high, v_low = split(tap_v)
            sums.append(
                lax.dot_general(
                    jnp.concatenate([v_high, v_low, v_high], axis=1),
                    jnp.concatenate([u_high, u_high, u_low], axis=1),
                    (((1,), (1,)), ((), ())),
                    preferred_element_type=F32,
                )
            )
        grid_ref[pl.ds(pl.multiple_of(j * TILE, TILE), TILE), :] = jnp.concatenate(sums, axis=1)
        return carry

    lax.fori_loop(0, NT, column, 0, unroll=32)
    strip = 16

    def transform(t, carry):
        base = pl.multiple_of(t * strip, strip)
        values = [grid_ref[pl.ds(pl.multiple_of(LANES * j + base, strip), strip), :] for j in range(COARSE)]
        table = twist_ref[pl.ds(base, strip), :]
        for q, (real, imag) in enumerate(real_transform(values)):
            c = table[:, q : q + 1]
            s = table[:, NT + q : NT + q + 1]
            if imag is None:
                turned = (real * c, real * s)
            else:
                turned = (real * c - imag * s, real * s + imag * c)
            for part in range(2):
                high, low = split(turned[part])
                high_ref[q, pl.ds(part * LANES + base, strip), :] = high
                low_ref[q, pl.ds(part * LANES + base, strip), :] = low
        return carry

    loads[0].wait()
    lax.fori_loop(0, LANES // strip, transform, 0, unroll=2)
    loads[1].wait()
    own = out_refs[0].shape[1] // STEP
    for q in range(HERM):
        high = high_ref[q]
        value = jnp.dot(
            matrix_ref[...], jnp.concatenate([high, low_ref[q], high], axis=0), preferred_element_type=F32
        )
        for peer, out_ref in enumerate(out_refs):
            for part in range(2):
                at = (peer * 4 + part) * own
                out_ref[part, pl.ds(q, own, stride=STEP), :] = value[at : at + own]
                if 0 < q < COARSE // 2:
                    at += 2 * own
                    out_ref[part, pl.ds(COARSE - q, own, stride=STEP), :] = value[at : at + own]


def ordered(who_ref, loaded):
    def exchanged(swap, x, y):
        return jnp.where(swap, y, x), jnp.where(swap, x, y)

    near, far = (exchanged(who_ref[1] == 1, *loaded[2 * e : 2 * e + 2]) for e in range(2))
    first, second = zip(*(exchanged(who_ref[0] == 1, near[core], far[core]) for core in range(2)))
    return [*first, *second]


def slabs_of(who_ref, piece_refs, rows):
    return list(zip(*(ordered(who_ref, [ref[part, rows, :] for ref in piece_refs]) for part in range(2))))


def strip_rows(t):
    per = COARSE // STRIP
    return pl.ds((t // per) * STEP + (t % per) * STRIP, STRIP)


def early_kernel(steps, who_ref, *rest):
    mine_ref, *piece_refs, turn_ref, out_ref, near_ref, landed = rest
    copies = [pltpu.make_async_copy(ref, near_ref.at[i], landed.at[i]) for i, ref in enumerate(piece_refs)]
    for copy in copies:
        copy.start()
    piece_refs = [near_ref.at[i] for i in range(len(copies))]

    def transform(t, carry):
        values = [(None, None)] * SLABS
        for i, k in enumerate(steps):
            for place, value in enumerate(slabs_of(
                who_ref, [mine_ref.at[k], *piece_refs[3 * i : 3 * i + 3]], strip_rows(t)
            )):
                values[place * (SLABS // 4) + k] = value
        base = pl.multiple_of(t * STRIP, STRIP)
        turned = [times(value, s / (2 * SLABS)) for s, value in enumerate(values)]
        for odd, chosen in enumerate((values, turned)):
            for k, (real, imag) in enumerate(complex_transform(chosen)):
                q = 2 * k + odd
                c, s = turn_ref[pl.ds(q, 1), :], turn_ref[pl.ds(COARSE + q, 1), :]
                out_ref[q, pl.ds(base, STRIP), :LANES] = real * c - imag * s
                out_ref[q, pl.ds(base, STRIP), LANES:] = real * s + imag * c
        return carry

    for copy in copies:
        copy.wait()
    lax.fori_loop(0, out_ref.shape[1] // STRIP, transform, 0)


def image_kernel(who_ref, early_ref, *rest):
    (mine_ref, *piece_refs), (matrix_ref, turn_ref, out_ref) = rest[:4], rest[4:7]
    piece_refs = [mine_ref.at[LAST], *piece_refs]
    fixed_ref, *blocked, landed, sent = rest[7:]
    highs, lows, stages, images = (blocked[i::4] for i in range(4))
    load = pltpu.make_async_copy(matrix_ref, fixed_ref, landed)
    load.start()
    own = piece_refs[-1].shape[1] // STEP

    def transform(block, g):
        t = block * groups + g
        values = slabs_of(who_ref, piece_refs, strip_rows(t))
        turned = [times(value, place / 8) for place, value in enumerate(values)]
        eight = [None] * 8
        for odd, chosen in enumerate((values, turned)):
            eight[odd::2] = complex_transform(chosen)
        from_rows, to_rows = (pl.ds(pl.multiple_of(x * STRIP, STRIP), STRIP) for x in (t, g))
        for q in range(COARSE):
            real, imag = eight[q % 8]
            c, s = turn_ref[pl.ds(q, 1), :], turn_ref[pl.ds(COARSE + q, 1), :]
            for part, value in enumerate((real * c - imag * s, real * s + imag * c)):
                lanes = slice(part * LANES, (part + 1) * LANES)
                high, low = split(early_ref[q, from_rows, lanes] + value)
                highs[block][q, to_rows, lanes] = high
                lows[block][q, to_rows, lanes] = low

    contract = (((1,), (1,)), ((), ()))
    blocks = COARSE * own // LANES
    groups = COARSE * own // STRIP // blocks
    width = G // groups

    def sums(block, g):
        for i in range(COARSE // groups):
            q = g * (COARSE // groups) + i
            both = lax.dot_general(fixed_ref[...], highs[block][q], contract, preferred_element_type=F32)
            more = lax.dot_general(fixed_ref[:LANES], lows[block][q], contract, preferred_element_type=F32)
            stages[block][pl.ds(q, LANES, stride=STEP), :] = both[:LANES] + both[LANES:] + more

    def leave(block, g):
        rows, lanes = pl.ds(block * LANES, LANES), pl.ds(pl.multiple_of(g * width, width), width)
        return pltpu.make_async_copy(images[block].at[:, lanes], out_ref.at[rows, lanes], sent.at[block, g])

    def turn(block, g):
        for t in range(width // LANES):
            first = g * (width // COARSE) + t * (LANES // COARSE)
            lanes = pl.ds(pl.multiple_of(g * width + t * LANES, LANES), LANES)
            value = jnp.concatenate(
                [stages[block][pl.ds((first + i) * STEP, COARSE), :] for i in range(LANES // COARSE)], axis=0
            )
            images[block][:, lanes] = value.T
        leave(block, g).start()

    for stage in range(blocks + 2):

        def body(g, carry, stage=stage):
            if stage < blocks:
                transform(stage, g)
            if 0 <= stage - 1 < blocks:
                sums(stage - 1, g)
            if 0 <= stage - 2 < blocks:
                turn(stage - 2, g)
            return carry

        if stage == 1:
            load.wait()
        lax.fori_loop(0, groups, body, 0)
    for block in range(blocks):
        for g in range(groups):
            leave(block, g).wait()


def constants(senders, own):
    cell = np.arange(LANES, dtype=np.float64)
    rows = []
    for peer in range(senders):
        for mirror in range(2):
            p = peer * own + np.arange(own)
            p = LANES - 1 - p if mirror else p
            phase = 2 * np.pi * ((p[:, None] * cell[None, :]) % LANES) / LANES
            sign = -1.0 if mirror else 1.0
            rows.append(np.concatenate([np.cos(phase), -np.sin(phase)], axis=1))
            rows.append(sign * np.concatenate([np.sin(phase), np.cos(phase)], axis=1))
    high, low = split_constant(np.concatenate(rows, axis=0))
    along_v = np.concatenate([high, high, low], axis=1).reshape(senders, 4 * own, 6 * LANES)
    phase = 2 * np.pi * ((np.arange(LANES)[:, None] * cell[None, :]) % LANES) / LANES
    support = (HALF + 1.0) ** 8
    scale = 1.0 / math.sqrt(senders * NT * NT * CAP) / support
    high, low = split_constant(scale * np.concatenate([np.cos(phase), -np.sin(phase)], axis=1))
    along_u = np.concatenate([high, low], axis=0)
    q = np.arange(COARSE)
    phase = 2 * np.pi * q[:, None] * cell[None, :] / G
    late = phase + 2 * np.pi * LAST * q[:, None] / COARSE
    turns = [np.concatenate([np.cos(x), np.sin(x)], axis=0).astype(np.float32) for x in (phase, late)]
    twist = np.zeros((LANES, 2 * NT))
    twist[:, :HERM] = np.cos(phase[:HERM]).T
    twist[:, NT : NT + HERM] = np.sin(phase[:HERM]).T
    return along_v, along_u, turns, twist.astype(np.float32)


def near(value):
    return pltpu.with_memory_space_constraint(value, pltpu.VMEM)


def far(value):
    return pltpu.with_memory_space_constraint(value, pltpu.HBM)


def fast_body(sample_weight, fraction_u, fraction_v, cell_code, tile_fill):
    group, inner = ("half", "low", "side", "chan"), ("low", "side", "chan")
    senders = lax.axis_size(group)
    own = LANES // senders
    steps, phases = SLABS // 4, 2
    along_v, along_u, turns, twist = constants(senders, own)
    packed = pl.pallas_call(
        pack_kernel,
        out_shape=[pltpu.HBM((senders, steps // phases, 6 * CAP, LANES), F32)] * phases,
        out_specs=[pl.BlockSpec(memory_space=pltpu.HBM)] * phases,
        in_specs=[pl.BlockSpec(memory_space=pltpu.HBM)] * 5,
        scratch_shapes=[
            pltpu.VMEM((3, NT, NT * CAP), F32),
            pltpu.VMEM((1, NT, NT * CAP), jnp.int32),
            pltpu.VMEM((1, NT, NT), jnp.int32),
            pltpu.VMEM((6, NT, LANES), F32),
            pltpu.VMEM((SLABS, 6 * CAP, LANES), F32),
            pltpu.SemaphoreType.DMA((senders * phases,)),
            pltpu.SemaphoreType.DMA((5,)),
        ],
        compiler_params=pltpu.CompilerParams(vmem_limit_bytes=6 * 1024 * 1024),
        name="pack",
    )(*map(far, (sample_weight, fraction_u, fraction_v, cell_code, tile_fill)))
    taps = [near(lax.all_to_all(part, group, split_axis=0, concat_axis=0, tiled=True)) for part in packed]

    chip = lax.axis_index(("half", "low", "side"))
    core = lax.axis_index("chan")

    def rows_of(chip, core):
        return lax.dynamic_index_in_dim(jnp.asarray(along_v), 2 * chip + core, 0, keepdims=False)

    def pairs_of(f):
        return [
            (4 * z + 2 * y + c, 4 * f(z, y, c)[0] + 2 * f(z, y, c)[1] + f(z, y, c)[2])
            for z in range(2)
            for y in range(2)
            for c in range(2)
        ]

    matrices = []
    for parity in range(2):
        other = chip ^ jnp.where((core + parity) % 2 == 0, 1, 2)
        matrices.append(
            jnp.concatenate(
                [rows_of(chip, core), rows_of(chip, 1 - core), rows_of(other, core), rows_of(other, 1 - core)], axis=0
            )
        )
    piece, whole = pltpu.VMEM((2, own * STEP, LANES), F32), pltpu.VMEM((steps, 2, own * STEP, LANES), F32)
    matrices = [far(matrix) for matrix in matrices]
    twist = far(jnp.asarray(twist))
    straights, crosseds, siblings = [], [], []
    for k in range(steps):
        phase, local = divmod(k, steps // phases)
        held = [] if k == 0 else [mine]
        run = pl.pallas_call(
            lambda *refs, k=k, local=local: grid_kernel(k, local, *refs),
            out_shape=[whole] + [piece] * 3,
            in_specs=[pl.BlockSpec(memory_space=pltpu.VMEM)]
            + [pl.BlockSpec(memory_space=pltpu.HBM)] * 2
            + [pl.BlockSpec(memory_space=pltpu.VMEM)] * len(held),
            out_specs=[pl.BlockSpec(memory_space=pltpu.VMEM)] * 4,
            input_output_aliases={3 + i: i for i in range(len(held))},
            scratch_shapes=[
                pltpu.VMEM((3, LANES, 2 * CAP * senders), F32),
                pltpu.VMEM((COARSE * LANES, LANES), F32),
                pltpu.VMEM((HERM, 2 * LANES, LANES), BF16),
                pltpu.VMEM((HERM, 2 * LANES, LANES), BF16),
                pltpu.VMEM((16 * own, 6 * LANES), BF16),
                pltpu.VMEM((LANES, 2 * NT), F32),
                pltpu.SemaphoreType.DMA((2,)),
            ],
            cost_estimate=pl.CostEstimate(flops=4_000_000_000, bytes_accessed=2_000_000, transcendentals=0),
            compiler_params=pltpu.CompilerParams(vmem_limit_bytes=8 * 1024 * 1024),
        )
        mine, sibling, straight, crossed = run(taps[phase], matrices[k % 2], twist, *held)

        def beside(z, y, c, swap, k=k):
            return (z, 1 - y, c ^ swap) if (k + c) % 2 == 0 else (1 - z, y, c ^ swap)

        straights.append(lax.ppermute(straight, inner, pairs_of(lambda z, y, c: beside(z, y, c, 0))))
        crosseds.append(lax.ppermute(crossed, inner, pairs_of(lambda z, y, c: beside(z, y, c, 1))))
        siblings.append(lax.ppermute(sibling, inner, pairs_of(lambda z, y, c: (z, y, 1 - c))))
    mine = near(mine)
    who = jnp.stack([lax.axis_index("low") ^ lax.axis_index("side"), core]).astype(jnp.int32)
    rows = COARSE * own
    first_steps = [k for k in range(steps) if k != LAST]
    run = pl.pallas_call(
        lambda *refs: early_kernel(first_steps, *refs),
        out_shape=pltpu.VMEM((COARSE, rows, 2 * LANES), F32),
        in_specs=[pl.BlockSpec(memory_space=pltpu.SMEM)]
        + [pl.BlockSpec(memory_space=pltpu.VMEM)]
        + [pl.BlockSpec(memory_space=pltpu.HBM)] * (3 * len(first_steps))
        + [pl.BlockSpec(memory_space=pltpu.VMEM)],
        out_specs=pl.BlockSpec(memory_space=pltpu.VMEM),
        scratch_shapes=[
            pltpu.VMEM((3 * len(first_steps), 2, own * STEP, LANES), F32),
            pltpu.SemaphoreType.DMA((3 * len(first_steps),)),
        ],
        compiler_params=pltpu.CompilerParams(vmem_limit_bytes=6 * 1024 * 1024),
        cost_estimate=pl.CostEstimate(flops=4_000_000_000, bytes_accessed=2_000_000, transcendentals=0),
        name="early",
    )
    early = run(
        who,
        mine,
        *[far(kind[k]) for k in first_steps for kind in (siblings, straights, crosseds)],
        near(jnp.asarray(turns[0])),
    )
    return pl.pallas_call(
        image_kernel,
        out_shape=jax.ShapeDtypeStruct((rows, G), F32),
        in_specs=[pl.BlockSpec(memory_space=pltpu.SMEM)] + [pl.BlockSpec(memory_space=pltpu.VMEM)] * 5
        + [pl.BlockSpec(memory_space=pltpu.HBM), pl.BlockSpec(memory_space=pltpu.VMEM)],
        out_specs=pl.BlockSpec(memory_space=pl.ANY),
        scratch_shapes=[
            pltpu.VMEM((2 * LANES, 2 * LANES), BF16),
            *[
                pltpu.VMEM((COARSE, LANES, 2 * LANES), BF16),
                pltpu.VMEM((COARSE, LANES, 2 * LANES), BF16),
                pltpu.VMEM((LANES * STEP, LANES), F32),
                pltpu.VMEM((LANES, G), F32),
            ]
            * (rows // LANES),
            pltpu.SemaphoreType.DMA(()),
            pltpu.SemaphoreType.DMA((rows // LANES, LANES // 16)),
        ],
        compiler_params=pltpu.CompilerParams(vmem_limit_bytes=20 * 1024 * 1024),
        name="image",
    )(
        who,
        early,
        mine,
        near(siblings[LAST]),
        near(straights[LAST]),
        near(crosseds[LAST]),
        far(jnp.asarray(along_u)),
        near(jnp.asarray(turns[1])),
    )


def solution(mesh):
    layouts, tiles, chans = (mesh.shape[name] for name in ("layout", "tile", "chan"))
    if (tiles, chans) == (HALVES * 4, 2) and LANES == 8 * tiles * chans:
        first = ("layout", "half", "low", "side", "chan")
        mesh, program = Mesh(mesh.devices.reshape(layouts, HALVES, 2, 2, chans), first), fast_body
    else:
        first, program = ("layout", "tile", "chan"), general_body
    step = jax.shard_map(
        program,
        mesh=mesh,
        in_specs=(P(first, None, None),) * 5,
        out_specs=P(first, None),
        check_vma=False,
    )
    if program is general_body:
        return step
    return step
```

profile of v0, /device:TPU:1, one launch (start us, length us, event | category | flops | bytes accessed | tf_op | source)
XLA Modules:
  0.0 75.7 jit_solution(6223670751958179181)
XLA Ops:
  0.0 3.0 %pack.1 = (f32[16,2,24,128]{3,2,1,0:T(8,128)}, f32[16,2,24,128]{3,2,1,0:T(8,128)}) custom-call(f32[1,64,256]{2,1,0:T(8,128)} %weight_ref.1, f32[1,64,256]{2,1,0:T(8,128)} %frac_u_ref.1, f32[1,64,256]{2,1,0:T(8,128)} %frac_v_ref.1, s32[1,64,256]{2,1,0:T(8,128)} %code_ref.1, s32[1,64,64]{2,1,0:T(8,128)} %fill_ref.1), custom_call_target="tpu_custom_call" | custom-call | tf_op jit(solution)/shard_map/pack/pallas_call | solution.py:529
  3.0 7.4 %all-to-all-start.1 = ((f32[16,2,24,128]{3,2,1,0:T(8,128)}), f32[16,2,24,128]{3,2,1,0:T(8,128)S(1)}, u32[]{:S(2)}, u32[]{:S(2)}) async-start(f32[16,2,24,128]{3,2,1,0:T(8,128)} %get-tuple-element.24), calls=%async_computation.1 | async-start | bytes 786432 | tf_op jit(solution)/shard_map/all_to_all | solution.py:546
  10.3 0.1 pad_add_fusion.refs_0_.who_ref
  10.4 0.9 %dynamic-slice_bitcast_fusion.1 = (bf16[32,768]{1,0:T(8,128)(2,1)S(1)}, bf16[32,768]{1,0:T(8,128)(2,1)S(1)}, bf16[32,768]{1,0:T(8,128)(2,1)S(1)}, bf16[32,768]{1...) fusion(bf16[16,32,768]{2,1,0:T(8,128)(2,1)} %constant.64.clone, s32[]{:T(128)S(6)} %select_n.47, ...), kind=kLoop, calls=%fused_computation.4 | loop fusion | bytes 589848 | tf_op jit(solution)/shard_map/jit(dynamic_index_in_dim)/squeeze | solution.py:552
  11.4 0.8 %pad_maximum_fusion.2 = (bf16[128,768]{1,0:T(8,128)(2,1)}, bf16[128,768]{1,0:T(8,128)(2,1)}) fusion(bf16[32,768]{1,0:T(8,128)(2,1)S(1)} %get-tuple-element.46, bf16[32,768]{1,0:T(8,128)(2,1)S(1)} %get-tuple-element.41, bf16[32,768]{1,0:T(8,128)(2,1)S(1)} %get-tuple-element.44, bf16[32,768]{1,0:T(8,128)(2,1)S(1)} %get-tuple-element.45, ...), kind=kLoop, calls=%fused_computation.2 | loop fusion | flops 1277952 | bytes 688128 | tf_op jit(solution)/shard_map/concatenate | solution.py:566
  12.1 10.1 %all-to-all-done.1.refs_0_ = f32[16,2,24,128]{3,2,1,0:T(8,128)S(1)} async-done(((f32[16,2,24,128]{3,2,1,0:T(8,128)}), f32[16,2,24,128]{3,2,1,0:T(8,128)S(1)}, u32[]{:S(2)}, u32[]{:S(2)}) %all-to-all-start.1) | async-done | bytes 393248 | tf_op jit(solution)/shard_map/all_to_all | solution.py:546
  22.2 3.7 %all-to-all-start = ((f32[16,2,24,128]{3,2,1,0:T(8,128)}), f32[16,2,24,128]{3,2,1,0:T(8,128)S(1)}, u32[]{:S(2)}, u32[]{:S(2)}) async-start(f32[16,2,24,128]{3,2,1,0:T(8,128)} %get-tuple-element.23), calls=%async_computation | async-start | bytes 786432 | tf_op jit(solution)/shard_map/all_to_all | solution.py:546
  25.9 5.6 %shard_map.100 = (f32[4,2,264,128]{3,2,1,0:T(8,128)S(1)}, f32[2,264,128]{2,1,0:T(8,128)S(1)}, f32[2,264,128]{2,1,0:T(8,128)S(1)}, f32[2,264,128]{2,1,0:T(8,128)S(1)}) custom-call(f32[16,2,24,128]{3,2,1,0:T(8,128)S(1)} %all-to-all-done.1.refs_0_, bf16[128,768]{1,0:T(8,128)(2,1)} %get-tuple-element.47.refs_1_, f32[128,128]{1,0:T(8,128)} %constant.65.clone.refs_2_), custom_call_target="tpu_custom_call" | custom-call | flops 4000000000 | bytes 2000000 | tf_op jit(solution)/shard_map/pallas_call | solution.py:597
  31.5 0.3 collective-permute-start
  31.8 1.5 %collective-permute-start.1 = (f32[2,264,128]{2,1,0:T(8,128)S(1)}, f32[2,264,128]{2,1,0:T(8,128)}, u32[]{:S(2)}, u32[]{:S(2)}) collective-permute-start(f32[2,264,128]{2,1,0:T(8,128)S(1)} %get-tuple-element.30), channel_id=1, source_target_pairs={{0,2},{1,5},{2,0},{3,7},{4,6},{5,1},{6,4},{7,3},{8,10},{9,13},{10,... | collective-permute-start | bytes 811016 | tf_op jit(solution)/shard_map/ppermute | solution.py:602
  33.3 1.5 %collective-permute-start.2 = (f32[2,264,128]{2,1,0:T(8,128)S(1)}, f32[2,264,128]{2,1,0:T(8,128)}, u32[]{:S(2)}, u32[]{:S(2)}) collective-permute-start(f32[2,264,128]{2,1,0:T(8,128)S(1)} %get-tuple-element.31), channel_id=1, source_target_pairs={{0,3},{1,4},{2,1},{3,6},{4,7},{5,0},{6,5},{7,2},{8,11},{9,12},{10,... | collective-permute-start | bytes 811016 | tf_op jit(solution)/shard_map/ppermute | solution.py:603
  34.8 5.6 %shard_map.101 = (f32[4,2,264,128]{3,2,1,0:T(8,128)S(1)}, f32[2,264,128]{2,1,0:T(8,128)S(1)}, f32[2,264,128]{2,1,0:T(8,128)S(1)}, f32[2,264,128]{2,1,0:T(8,128)S(1)}) custom-call(f32[16,2,24,128]{3,2,1,0:T(8,128)S(1)} %all-to-all-done.1.refs_0_, bf16[128,768]{1,0:T(8,128)(2,1)} %get-tuple-element.48.refs_1_, ...), custom_call_target="tpu_custom_call", output_to_operand_aliasing={{0}: (3, {})} | custom-call | flops 4000000000 | bytes 2000000 | tf_op jit(solution)/shard_map/pallas_call | solution.py:597
  40.4 0.2 collective-permute-start.3
  40.6 0.3 collective-permute-start.4
  40.8 0.0 all-to-all-done.refs_0_
  40.8 5.6 %shard_map.102 = (f32[4,2,264,128]{3,2,1,0:T(8,128)S(1)}, f32[2,264,128]{2,1,0:T(8,128)S(1)}, f32[2,264,128]{2,1,0:T(8,128)S(1)}, f32[2,264,128]{2,1,0:T(8,128)S(1)}) custom-call(f32[16,2,24,128]{3,2,1,0:T(8,128)S(1)} %all-to-all-done.refs_0_, bf16[128,768]{1,0:T(8,128)(2,1)} %get-tuple-element.47.refs_1_, ...), custom_call_target="tpu_custom_call", output_to_operand_aliasing={{0}: (3, {})} | custom-call | flops 4000000000 | bytes 2000000 | tf_op jit(solution)/shard_map/pallas_call | solution.py:597
  46.4 0.0 collective-permute-done.refs_2_
  46.4 0.7 collective-permute-start.5
  47.1 0.0 collective-permute-done.1.refs_3_
  47.1 0.1 collective-permute-start.6
  47.2 0.0 collective-permute-done.2.refs_4_
  47.2 1.3 %collective-permute-start.7 = (f32[2,264,128]{2,1,0:T(8,128)S(1)}, f32[2,264,128]{2,1,0:T(8,128)S(1)}, u32[]{:S(2)}, u32[]{:S(2)}) collective-permute-start(f32[2,264,128]{2,1,0:T(8,128)S(1)} %get-tuple-element.36), channel_id=1, source_target_pairs={{0,2},{1,5},{2,0},{3,7},{4,6},{5,1},{6,4},{7,3},{8,10},{9,13},{10,... | collective-permute-start | bytes 811016 | tf_op jit(solution)/shard_map/ppermute | solution.py:602
  48.6 0.0 collective-permute-done.3.refs_5_
  48.6 1.8 %collective-permute-start.8 = (f32[2,264,128]{2,1,0:T(8,128)S(1)}, f32[2,264,128]{2,1,0:T(8,128)S(1)}, u32[]{:S(2)}, u32[]{:S(2)}) collective-permute-start(f32[2,264,128]{2,1,0:T(8,128)S(1)} %get-tuple-element.37), channel_id=1, source_target_pairs={{0,3},{1,4},{2,1},{3,6},{4,7},{5,0},{6,5},{7,2},{8,11},{9,12},{10,... | collective-permute-start | bytes 811016 | tf_op jit(solution)/shard_map/ppermute | solution.py:603
  50.4 0.0 copy-start.1
  50.4 5.6 %shard_map.103 = (f32[4,2,264,128]{3,2,1,0:T(8,128)S(1)}, f32[2,264,128]{2,1,0:T(8,128)S(1)}, f32[2,264,128]{2,1,0:T(8,128)S(1)}, f32[2,264,128]{2,1,0:T(8,128)S(1)}) custom-call(f32[16,2,24,128]{3,2,1,0:T(8,128)S(1)} %all-to-all-done.refs_0_, bf16[128,768]{1,0:T(8,128)(2,1)} %get-tuple-element.48.refs_1_, ...), custom_call_target="tpu_custom_call", output_to_operand_aliasing={{0}: (3, {})} | custom-call | flops 4000000000 | bytes 2000000 | tf_op jit(solution)/shard_map/pallas_call | solution.py:597
  55.9 0.0 collective-permute-done.4.refs_6_
  55.9 0.1 collective-permute-start.9
  56.0 0.0 collective-permute-done.5.refs_7_
  56.0 0.0 copy-start.2
  56.0 0.3 collective-permute-start.10
  56.4 0.0 collective-permute-done.6.refs_8_
  56.4 0.0 copy-start.3
  56.4 0.7 collective-permute-start.11
  57.1 0.0 collective-permute-done.7.refs_9_
  57.1 0.0 copy-start.4
  57.1 1.3 %collective-permute-done.8.refs_10_ = f32[2,264,128]{2,1,0:T(8,128)S(1)} collective-permute-done((f32[2,264,128]{2,1,0:T(8,128)S(1)}, f32[2,264,128]{2,1,0:T(8,128)S(1)}, u32[]{:S(2)}, u32[]{:S(2)}) %collective-permute-start.8) | collective-permute-done | bytes 270368 | tf_op jit(solution)/shard_map/ppermute | solution.py:603
  58.4 0.0 copy-done.2
  58.4 0.0 copy-done.3
  58.4 0.0 copy-done.4
  58.4 0.7 copy-done.5
  59.1 0.0 copy-done.1
  59.1 5.1 %early.1.early_ref = f32[32,256,256]{2,1,0:T(8,128)S(1)} custom-call(s32[2]{0:T(128)S(1)} %pad_add_fusion.refs_0_.who_ref, f32[4,2,264,128]{3,2,1,0:T(8,128)S(1)} %get-tuple-element.28.refs_1_.rest_0_, f32[2,264,128]{2,1,0:T(8,128)} %collective-permute-done.refs_2_, f32[2,264,128]{2,1,0:T(8,128)} %collective-permute-done.1.refs_3_, ...), custom_call_target="tpu_custom_call" | custom-call | flops 4000000000 | bytes 2000000 | tf_op jit(solution)/shard_map/early/pallas_call | solution.py:625
  64.3 0.0 collective-permute-done.9.rest_1_
  64.3 0.0 collective-permute-done.10.rest_2_
  64.3 0.9 %collective-permute-done.11.rest_3_ = f32[2,264,128]{2,1,0:T(8,128)S(1)} collective-permute-done((f32[2,264,128]{2,1,0:T(8,128)S(1)}, f32[2,264,128]{2,1,0:T(8,128)S(1)}, u32[]{:S(2)}, u32[]{:S(2)}) %collective-permute-start.11) | collective-permute-done | bytes 270368 | tf_op jit(solution)/shard_map/ppermute | solution.py:603
  65.2 0.0 copy-done
  65.2 10.3 %image.1 = f32[256,4096]{1,0:T(8,128)} custom-call(s32[2]{0:T(128)S(1)} %pad_add_fusion.refs_0_.who_ref, f32[32,256,256]{2,1,0:T(8,128)S(1)} %early.1.early_ref, f32[4,2,264,128]{3,2,1,0:T(8,128)S(1)} %get-tuple-element.28.refs_1_.rest_0_, f32[2,264,128]{2,1,0:T(8,128)S(1)} %collective-permute-done.9.rest_1_, ...), custom_call_target="tpu_custom_call" | custom-call | tf_op jit(solution)/shard_map/image/pallas_call | solution.py:631
  (2 shorter events, 0.0 us)
Async XLA Ops:
  3.0 19.2 %all-to-all-start.1 = ((f32[16,2,24,128]{3,2,1,0:T(8,128)}), f32[16,2,24,128]{3,2,1,0:T(8,128)S(1)}, u32[]{:S(2)}, u32[]{:S(2)}) async-start(f32[16,2,24,128]{3,2,1,0:T(8,128)} %get-tuple-element.24), calls=%async_computation.1 | async-start | bytes 786432 | tf_op jit(solution)/shard_map/all_to_all | solution.py:546
  22.2 18.6 %all-to-all-start = ((f32[16,2,24,128]{3,2,1,0:T(8,128)}), f32[16,2,24,128]{3,2,1,0:T(8,128)S(1)}, u32[]{:S(2)}, u32[]{:S(2)}) async-start(f32[16,2,24,128]{3,2,1,0:T(8,128)} %get-tuple-element.23), calls=%async_computation | async-start | bytes 786432 | tf_op jit(solution)/shard_map/all_to_all | solution.py:546
  31.5 14.9 %collective-permute-start = (f32[2,264,128]{2,1,0:T(8,128)S(1)}, f32[2,264,128]{2,1,0:T(8,128)}, u32[]{:S(2)}, u32[]{:S(2)}) collective-permute-start(f32[2,264,128]{2,1,0:T(8,128)S(1)} %get-tuple-element.29), channel_id=1, source_target_pairs={{0,1},{1,0},{2,3},{3,2},{4,5},{5,4},{6,7},{7,6},{8,9},{9,8},{10,11... | collective-permute-start | bytes 811016 | tf_op jit(solution)/shard_map/ppermute | solution.py:604
  31.8 15.3 %collective-permute-start.1 = (f32[2,264,128]{2,1,0:T(8,128)S(1)}, f32[2,264,128]{2,1,0:T(8,128)}, u32[]{:S(2)}, u32[]{:S(2)}) collective-permute-start(f32[2,264,128]{2,1,0:T(8,128)S(1)} %get-tuple-element.30), channel_id=1, source_target_pairs={{0,2},{1,5},{2,0},{3,7},{4,6},{5,1},{6,4},{7,3},{8,10},{9,13},{10,... | collective-permute-start | bytes 811016 | tf_op jit(solution)/shard_map/ppermute | solution.py:602
  33.3 13.9 %collective-permute-start.2 = (f32[2,264,128]{2,1,0:T(8,128)S(1)}, f32[2,264,128]{2,1,0:T(8,128)}, u32[]{:S(2)}, u32[]{:S(2)}) collective-permute-start(f32[2,264,128]{2,1,0:T(8,128)S(1)} %get-tuple-element.31), channel_id=1, source_target_pairs={{0,3},{1,4},{2,1},{3,6},{4,7},{5,0},{6,5},{7,2},{8,11},{9,12},{10,... | collective-permute-start | bytes 811016 | tf_op jit(solution)/shard_map/ppermute | solution.py:603
  40.4 8.2 %collective-permute-start.3 = (f32[2,264,128]{2,1,0:T(8,128)S(1)}, f32[2,264,128]{2,1,0:T(8,128)}, u32[]{:S(2)}, u32[]{:S(2)}) collective-permute-start(f32[2,264,128]{2,1,0:T(8,128)S(1)} %get-tuple-element.32), channel_id=1, source_target_pairs={{0,1},{1,0},{2,3},{3,2},{4,5},{5,4},{6,7},{7,6},{8,9},{9,8},{10,11... | collective-permute-start | bytes 811016 | tf_op jit(solution)/shard_map/ppermute | solution.py:604
  40.6 15.4 %collective-permute-start.4 = (f32[2,264,128]{2,1,0:T(8,128)S(1)}, f32[2,264,128]{2,1,0:T(8,128)}, u32[]{:S(2)}, u32[]{:S(2)}) collective-permute-start(f32[2,264,128]{2,1,0:T(8,128)S(1)} %get-tuple-element.33), channel_id=1, source_target_pairs={{0,4},{1,3},{2,6},{3,1},{4,0},{5,7},{6,2},{7,5},{8,12},{9,11},{10,... | collective-permute-start | bytes 811016 | tf_op jit(solution)/shard_map/ppermute | solution.py:602
  46.4 9.6 %collective-permute-start.5 = (f32[2,264,128]{2,1,0:T(8,128)S(1)}, f32[2,264,128]{2,1,0:T(8,128)S(1)}, u32[]{:S(2)}, u32[]{:S(2)}) collective-permute-start(f32[2,264,128]{2,1,0:T(8,128)S(1)} %get-tuple-element.34), channel_id=1, source_target_pairs={{0,5},{1,2},{2,7},{3,0},{4,1},{5,6},{6,3},{7,4},{8,13},{9,10},{10,... | collective-permute-start | bytes 811016 | tf_op jit(solution)/shard_map/ppermute | solution.py:603
  47.1 9.3 %collective-permute-start.6 = (f32[2,264,128]{2,1,0:T(8,128)S(1)}, f32[2,264,128]{2,1,0:T(8,128)S(1)}, u32[]{:S(2)}, u32[]{:S(2)}) collective-permute-start(f32[2,264,128]{2,1,0:T(8,128)S(1)} %get-tuple-element.35), channel_id=1, source_target_pairs={{0,1},{1,0},{2,3},{3,2},{4,5},{5,4},{6,7},{7,6},{8,9},{9,8},{10,11... | collective-permute-start | bytes 811016 | tf_op jit(solution)/shard_map/ppermute | solution.py:604
  47.2 9.8 %collective-permute-start.7 = (f32[2,264,128]{2,1,0:T(8,128)S(1)}, f32[2,264,128]{2,1,0:T(8,128)S(1)}, u32[]{:S(2)}, u32[]{:S(2)}) collective-permute-start(f32[2,264,128]{2,1,0:T(8,128)S(1)} %get-tuple-element.36), channel_id=1, source_target_pairs={{0,2},{1,5},{2,0},{3,7},{4,6},{5,1},{6,4},{7,3},{8,10},{9,13},{10,... | collective-permute-start | bytes 811016 | tf_op jit(solution)/shard_map/ppermute | solution.py:602
  48.6 9.8 %collective-permute-start.8 = (f32[2,264,128]{2,1,0:T(8,128)S(1)}, f32[2,264,128]{2,1,0:T(8,128)S(1)}, u32[]{:S(2)}, u32[]{:S(2)}) collective-permute-start(f32[2,264,128]{2,1,0:T(8,128)S(1)} %get-tuple-element.37), channel_id=1, source_target_pairs={{0,3},{1,4},{2,1},{3,6},{4,7},{5,0},{6,5},{7,2},{8,11},{9,12},{10,... | collective-permute-start | bytes 811016 | tf_op jit(solution)/shard_map/ppermute | solution.py:603
  50.4 8.7 %copy-start.1 = (f32[64,128]{1,0:T(8,128)S(1)}, f32[64,128]{1,0:T(8,128)}, u32[]{:S(2)}) copy-start(f32[64,128]{1,0:T(8,128)} %constant.66.clone.refs_11_) | copy-start | bytes 98308
  55.9 8.3 %collective-permute-start.9 = (f32[2,264,128]{2,1,0:T(8,128)S(1)}, f32[2,264,128]{2,1,0:T(8,128)S(1)}, u32[]{:S(2)}, u32[]{:S(2)}) collective-permute-start(f32[2,264,128]{2,1,0:T(8,128)S(1)} %get-tuple-element.38), channel_id=1, source_target_pairs={{0,1},{1,0},{2,3},{3,2},{4,5},{5,4},{6,7},{7,6},{8,9},{9,8},{10,11... | collective-permute-start | bytes 811016 | tf_op jit(solution)/shard_map/ppermute | solution.py:604
  56.0 2.4 %copy-start.2 = (f32[2,264,128]{2,1,0:T(8,128)}, f32[2,264,128]{2,1,0:T(8,128)S(1)}, u32[]{:S(2)}) copy-start(f32[2,264,128]{2,1,0:T(8,128)S(1)} %collective-permute-done.5.refs_7_) | copy-start | bytes 811012
  56.0 8.2 %collective-permute-start.10 = (f32[2,264,128]{2,1,0:T(8,128)S(1)}, f32[2,264,128]{2,1,0:T(8,128)S(1)}, u32[]{:S(2)}, u32[]{:S(2)}) collective-permute-start(f32[2,264,128]{2,1,0:T(8,128)S(1)} %get-tuple-element.39), channel_id=1, source_target_pairs={{0,4},{1,3},{2,6},{3,1},{4,0},{5,7},{6,2},{7,5},{8,12},{9,11},{10,... | collective-permute-start | bytes 811016 | tf_op jit(solution)/shard_map/ppermute | solution.py:602
  56.4 2.0 %copy-start.3 = (f32[2,264,128]{2,1,0:T(8,128)}, f32[2,264,128]{2,1,0:T(8,128)S(1)}, u32[]{:S(2)}) copy-start(f32[2,264,128]{2,1,0:T(8,128)S(1)} %collective-permute-done.6.refs_8_) | copy-start | bytes 811012
  56.4 8.8 %collective-permute-start.11 = (f32[2,264,128]{2,1,0:T(8,128)S(1)}, f32[2,264,128]{2,1,0:T(8,128)S(1)}, u32[]{:S(2)}, u32[]{:S(2)}) collective-permute-start(f32[2,264,128]{2,1,0:T(8,128)S(1)} %get-tuple-element.40), channel_id=1, source_target_pairs={{0,5},{1,2},{2,7},{3,0},{4,1},{5,6},{6,3},{7,4},{8,13},{9,10},{10,... | collective-permute-start | bytes 811016 | tf_op jit(solution)/shard_map/ppermute | solution.py:603
  57.1 1.4 %copy-start.4 = (f32[2,264,128]{2,1,0:T(8,128)}, f32[2,264,128]{2,1,0:T(8,128)S(1)}, u32[]{:S(2)}) copy-start(f32[2,264,128]{2,1,0:T(8,128)S(1)} %collective-permute-done.7.refs_9_) | copy-start | bytes 811012
  58.4 0.7 copy-start.5
  59.1 6.1 %copy-start = (f32[64,128]{1,0:T(8,128)S(1)}, f32[64,128]{1,0:T(8,128)}, u32[]{:S(2)}) copy-start(f32[64,128]{1,0:T(8,128)} %constant.68.clone.rest_5_) | copy-start | bytes 98308
where the time goes:
time: 76.1 us; the launch traced here: 75.7 us
  Pallas kernels  40.6 us (53%)
  starting transfers between devices  19.9 us (26%)
  waiting for transfers between devices  12.4 us (16%)
  local copies, waits for them, and re-layouts  1.65 us (2%)
  other arithmetic  0.85 us (1%)
    pallas_call x4, Pallas kernels, fast_body(): run(taps[phase], matrices[k % 2], twist, *held)  22.2 us
    all_to_all x2, starting transfers between devices, fast_body(): lax.all_to_all(part, group, split_axis=0, concat_axis=0, tiled=True)  11.1 us
    pallas_call x1, Pallas kernels, fast_body(): pl.pallas_call(image_kernel, out_shape=jax.ShapeDtypeStruct((rows, G), F3...  10.3 us
    all_to_all x2, waiting for transfers between devices, fast_body(): lax.all_to_all(part, group, split_axis=0, concat_axis=0, tiled=True)  10.1 us
    pallas_call x1, Pallas kernels, fast_body(): run(who, mine, *[far(kind[k]) for k in first_steps for kind in (siblings,...  5.14 us
    ppermute x4, starting transfers between devices, fast_body(): lax.ppermute(crossed, inner, pairs_of(lambda z, y, c: beside(z, y, c, 1)))  4.66 us
    ppermute x4, starting transfers between devices, fast_body(): lax.ppermute(straight, inner, pairs_of(lambda z, y, c: beside(z, y, c, 0)))  3.5 us
    pallas_call x1, Pallas kernels, fast_body(): pl.pallas_call(pack_kernel, out_shape=[pltpu.HBM((senders, steps // phase...  2.98 us
  transfers between devices with their start and end apart: 14, of which 3 were waited for; matrix products, arithmetic and copies ran while one was open for 2% of the time, Pallas kernels for 36%

commit v1 on v0

--- a/solution.py
+++ b/solution.py
@@ -291,7 +291,10 @@
 
 def grid_kernel(k, local, taps_ref, matrix_from, twist_from, *rest):
     *refs, place_ref, grid_ref, high_ref, low_ref, matrix_ref, twist_ref, landed = rest
-    out_refs = [refs[-4].at[k], *refs[-3:]]
+    if k == LAST:
+        out_refs = [refs[-4].at[k], *refs[-3:]]
+    else:
+        out_refs = [refs[-3].at[k], refs[-2], refs[-1].at[0], refs[-1].at[1]]
     loads = [
         pltpu.make_async_copy(twist_from, twist_ref, landed.at[0]),
         pltpu.make_async_copy(matrix_from, matrix_ref, landed.at[1]),
@@ -386,7 +389,8 @@
 
 def early_kernel(steps, who_ref, *rest):
     mine_ref, *piece_refs, turn_ref, out_ref, near_ref, landed = rest
-    copies = [pltpu.make_async_copy(ref, near_ref.at[i], landed.at[i]) for i, ref in enumerate(piece_refs)]
+    sources = [ref if i % 3 == 0 else ref.at[i % 3 - 1] for i, ref in enumerate(piece_refs)]
+    copies = [pltpu.make_async_copy(ref, near_ref.at[i], landed.at[i]) for i, ref in enumerate(sources)]
     for copy in copies:
         copy.start()
     piece_refs = [near_ref.at[i] for i in range(len(copies))]
@@ -567,6 +571,7 @@
                 [rows_of(chip, core), rows_of(chip, 1 - core), rows_of(other, core), rows_of(other, 1 - core)], axis=0
             )
         )
+    double = pltpu.VMEM((2, 2, own * STEP, LANES), F32)
     piece, whole = pltpu.VMEM((2, own * STEP, LANES), F32), pltpu.VMEM((steps, 2, own * STEP, LANES), F32)
     matrices = [far(matrix) for matrix in matrices]
     twist = far(jnp.asarray(twist))
@@ -576,11 +581,11 @@
         held = [] if k == 0 else [mine]
         run = pl.pallas_call(
             lambda *refs, k=k, local=local: grid_kernel(k, local, *refs),
-            out_shape=[whole] + [piece] * 3,
+            out_shape=[whole] + ([piece] * 3 if k == LAST else [piece, double]),
             in_specs=[pl.BlockSpec(memory_space=pltpu.VMEM)]
             + [pl.BlockSpec(memory_space=pltpu.HBM)] * 2
             + [pl.BlockSpec(memory_space=pltpu.VMEM)] * len(held),
-            out_specs=[pl.BlockSpec(memory_space=pltpu.VMEM)] * 4,
+            out_specs=[pl.BlockSpec(memory_space=pltpu.VMEM)] * (4 if k == LAST else 3),
             input_output_aliases={3 + i: i for i in range(len(held))},
             scratch_shapes=[
                 pltpu.VMEM((3, LANES, 2 * CAP * senders), F32),
@@ -594,13 +599,16 @@
             cost_estimate=pl.CostEstimate(flops=4_000_000_000, bytes_accessed=2_000_000, transcendentals=0),
             compiler_params=pltpu.CompilerParams(vmem_limit_bytes=8 * 1024 * 1024),
         )
-        mine, sibling, straight, crossed = run(taps[phase], matrices[k % 2], twist, *held)
+        mine, sibling, straight, *crossed = run(taps[phase], matrices[k % 2], twist, *held)
 
         def beside(z, y, c, swap, k=k):
             return (z, 1 - y, c ^ swap) if (k + c) % 2 == 0 else (1 - z, y, c ^ swap)
 
         straights.append(lax.ppermute(straight, inner, pairs_of(lambda z, y, c: beside(z, y, c, 0))))
-        crosseds.append(lax.ppermute(crossed, inner, pairs_of(lambda z, y, c: beside(z, y, c, 1))))
+        if k == LAST:
+            crosseds.append(lax.ppermute(crossed[0], inner, pairs_of(lambda z, y, c: beside(z, y, c, 1))))
+        else:
+            crosseds.append(lax.ppermute(straights[k], inner, pairs_of(lambda z, y, c: (z, y, 1 - c))))
         siblings.append(lax.ppermute(sibling, inner, pairs_of(lambda z, y, c: (z, y, 1 - c))))
     mine = near(mine)
     who = jnp.stack([lax.axis_index("low") ^ lax.axis_index("side"), core]).astype(jnp.int32)

time: 76.1 us -> 84 us (1.10)
  the two profiles are of different devices: /device:TPU:1 before, /device:TPU:13 now
where the time goes in v1:
time: 84 us; the launch traced here: 82.6 us
  Pallas kernels  40.5 us (48%)
  waiting for transfers between devices  20.2 us (24%)
  starting transfers between devices  19.2 us (23%)
  local copies, waits for them, and re-layouts  1.73 us (2%)
  other arithmetic  0.86 us (1%)
    pallas_call x4, Pallas kernels, fast_body(): run(taps[phase], matrices[k % 2], twist, *held)  22.2 us
    all_to_all x2, starting transfers between devices, fast_body(): lax.all_to_all(part, group, split_axis=0, concat_axis=0, tiled=True)  11.4 us
    pallas_call x1, Pallas kernels, fast_body(): pl.pallas_call(image_kernel, out_shape=jax.ShapeDtypeStruct((rows, G), F3...  10.2 us
    all_to_all x2, waiting for transfers between devices, fast_body(): lax.all_to_all(part, group, split_axis=0, concat_axis=0, tiled=True)  9.04 us
    ppermute x4, waiting for transfers between devices, fast_body(): lax.ppermute(straight, inner, pairs_of(lambda z, y, c: beside(z, y, c, 0)))  8.99 us
    pallas_call x1, Pallas kernels, fast_body(): run(who, mine, *[far(kind[k]) for k in first_steps for kind in (siblings,...  5.1 us
    ppermute x3, starting transfers between devices, fast_body(): lax.ppermute(straights[k], inner, pairs_of(lambda z, y, c: (z, y, 1 - c)))  3.02 us
    pallas_call x1, Pallas kernels, fast_body(): pl.pallas_call(pack_kernel, out_shape=[pltpu.HBM((senders, steps // phase...  2.99 us
  transfers between devices with their start and end apart: 14, of which 4 were waited for; matrix products, arithmetic and copies ran while one was open for 2% of the time, Pallas kernels for 33%

profile of v1, /device:TPU:13, one launch (start us, length us, event | category | flops | bytes accessed | tf_op | source)
XLA Modules:
  0.0 82.6 jit_solution(15945884918961016294)
XLA Ops:
  0.0 3.0 %pack.1 = (f32[16,2,24,128]{3,2,1,0:T(8,128)}, f32[16,2,24,128]{3,2,1,0:T(8,128)}) custom-call(f32[1,64,256]{2,1,0:T(8,128)} %weight_ref.1, f32[1,64,256]{2,1,0:T(8,128)} %frac_u_ref.1, f32[1,64,256]{2,1,0:T(8,128)} %frac_v_ref.1, s32[1,64,256]{2,1,0:T(8,128)} %code_ref.1, s32[1,64,64]{2,1,0:T(8,128)} %fill_ref.1), custom_call_target="tpu_custom_call" | custom-call | tf_op jit(solution)/shard_map/pack/pallas_call | solution.py:533
  3.0 6.5 %all-to-all-start.1 = ((f32[16,2,24,128]{3,2,1,0:T(8,128)}), f32[16,2,24,128]{3,2,1,0:T(8,128)S(1)}, u32[]{:S(2)}, u32[]{:S(2)}) async-start(f32[16,2,24,128]{3,2,1,0:T(8,128)} %get-tuple-element.21), calls=%async_computation.1 | async-start | bytes 786432 | tf_op jit(solution)/shard_map/all_to_all | solution.py:550
  9.5 0.9 %dynamic-slice_bitcast_fusion.1 = (bf16[32,768]{1,0:T(8,128)(2,1)S(1)}, bf16[32,768]{1,0:T(8,128)(2,1)S(1)}, bf16[32,768]{1,0:T(8,128)(2,1)S(1)}, bf16[32,768]{1...) fusion(bf16[16,32,768]{2,1,0:T(8,128)(2,1)} %constant.64.clone, s32[]{:T(128)S(6)} %select_n.47, ...), kind=kLoop, calls=%fused_computation.4 | loop fusion | bytes 589848 | tf_op jit(solution)/shard_map/jit(dynamic_index_in_dim)/squeeze | solution.py:556
  10.5 0.8 pad_maximum_fusion.2
  11.3 9.0 %all-to-all-done.1.refs_0_ = f32[16,2,24,128]{3,2,1,0:T(8,128)S(1)} async-done(((f32[16,2,24,128]{3,2,1,0:T(8,128)}), f32[16,2,24,128]{3,2,1,0:T(8,128)S(1)}, u32[]{:S(2)}, u32[]{:S(2)}) %all-to-all-start.1) | async-done | bytes 393248 | tf_op jit(solution)/shard_map/all_to_all | solution.py:550
  20.3 4.9 %all-to-all-start = ((f32[16,2,24,128]{3,2,1,0:T(8,128)}), f32[16,2,24,128]{3,2,1,0:T(8,128)S(1)}, u32[]{:S(2)}, u32[]{:S(2)}) async-start(f32[16,2,24,128]{3,2,1,0:T(8,128)} %get-tuple-element.20), calls=%async_computation | async-start | bytes 786432 | tf_op jit(solution)/shard_map/all_to_all | solution.py:550
  25.2 5.6 %shard_map.100 = (f32[4,2,264,128]{3,2,1,0:T(8,128)S(1)}, f32[2,264,128]{2,1,0:T(8,128)S(1)}, f32[2,2,264,128]{3,2,1,0:T(8,128)S(1)}) custom-call(f32[16,2,24,128]{3,2,1,0:T(8,128)S(1)} %all-to-all-done.1.refs_0_, bf16[128,768]{1,0:T(8,128)(2,1)} %get-tuple-element.41.refs_1_, f32[128,128]{1,0:T(8,128)} %constant.65.clone.refs_2_), custom_call_target="tpu_custom_call" | custom-call | flops 4000000000 | bytes 2000000 | tf_op jit(solution)/shard_map/pallas_call | solution.py:602
  30.7 5.6 %shard_map.101 = (f32[4,2,264,128]{3,2,1,0:T(8,128)S(1)}, f32[2,264,128]{2,1,0:T(8,128)S(1)}, f32[2,2,264,128]{3,2,1,0:T(8,128)S(1)}) custom-call(f32[16,2,24,128]{3,2,1,0:T(8,128)S(1)} %all-to-all-done.1.refs_0_, bf16[128,768]{1,0:T(8,128)(2,1)} %get-tuple-element.42.refs_1_, f32[128,128]{1,0:T(8,128)} %constant.65.clone.refs_2_, ...), custom_call_target="tpu_custom_call", output_to_operand_aliasing={{0}: (3, {})} | custom-call | flops 4000000000 | bytes 2000000 | tf_op jit(solution)/shard_map/pallas_call | solution.py:602
  36.3 0.3 collective-permute-start.4
  36.6 0.1 collective-permute-start.1
  36.7 0.0 all-to-all-done.refs_0_
  36.7 5.6 %shard_map.102 = (f32[4,2,264,128]{3,2,1,0:T(8,128)S(1)}, f32[2,264,128]{2,1,0:T(8,128)S(1)}, f32[2,2,264,128]{3,2,1,0:T(8,128)S(1)}) custom-call(f32[16,2,24,128]{3,2,1,0:T(8,128)S(1)} %all-to-all-done.refs_0_, bf16[128,768]{1,0:T(8,128)(2,1)} %get-tuple-element.41.refs_1_, f32[128,128]{1,0:T(8,128)} %constant.65.clone.refs_2_, ...), custom_call_target="tpu_custom_call", output_to_operand_aliasing={{0}: (3, {})} | custom-call | flops 4000000000 | bytes 2000000 | tf_op jit(solution)/shard_map/pallas_call | solution.py:602
  42.3 1.4 %collective-permute-start.7 = (f32[2,2,264,128]{3,2,1,0:T(8,128)S(1)}, f32[2,2,264,128]{3,2,1,0:T(8,128)}, u32[]{:S(2)}, u32[]{:S(2)}) collective-permute-start(f32[2,2,264,128]{3,2,1,0:T(8,128)S(1)} %get-tuple-element.31), channel_id=1, source_target_pairs={{0,2},{1,5},{2,0},{3,7},{4,6},{5,1},{6,4},{7,3},{8,10},{9,13},{10,... | collective-permute-start | bytes 1622024 | tf_op jit(solution)/shard_map/ppermute | solution.py:607
  43.7 1.2 %collective-permute-start = (f32[2,264,128]{2,1,0:T(8,128)S(1)}, f32[2,264,128]{2,1,0:T(8,128)}, u32[]{:S(2)}, u32[]{:S(2)}) collective-permute-start(f32[2,264,128]{2,1,0:T(8,128)S(1)} %get-tuple-element.26), channel_id=1, source_target_pairs={{0,1},{1,0},{2,3},{3,2},{4,5},{5,4},{6,7},{7,6},{8,9},{9,8},{10,11... | collective-permute-start | bytes 811016 | tf_op jit(solution)/shard_map/ppermute | solution.py:612
  44.9 4.4 %collective-permute-done.4.refs_6_ = f32[2,2,264,128]{3,2,1,0:T(8,128)} collective-permute-done((f32[2,2,264,128]{3,2,1,0:T(8,128)S(1)}, f32[2,2,264,128]{3,2,1,0:T(8,128)}, u32[]{:S(2)}, u32[]{:S(2)}) %collective-permute-start.4) | collective-permute-done | bytes 540704 | tf_op jit(solution)/shard_map/ppermute | solution.py:607
  49.4 2.6 %collective-permute-start.5 = (f32[2,2,264,128]{3,2,1,0:T(8,128)}, f32[2,2,264,128]{3,2,1,0:T(8,128)S(1)}, u32[]{:S(2)}, u32[]{:S(2)}) collective-permute-start(f32[2,2,264,128]{3,2,1,0:T(8,128)} %collective-permute-done.4.refs_6_), channel_id=1, source_target_pairs={{0,1},{1,0},{2,3},{3,2},{4,5},{5,4},{6,7},{7,6},{8,9},{9,8},{10,11... | collective-permute-start | bytes 1622024 | tf_op jit(solution)/shard_map/ppermute | solution.py:611
  52.0 0.0 collective-permute-done.1.refs_3_
  52.0 0.0 collective-permute-start.2
  52.0 4.5 %collective-permute-done.7.refs_9_ = f32[2,2,264,128]{3,2,1,0:T(8,128)} collective-permute-done((f32[2,2,264,128]{3,2,1,0:T(8,128)S(1)}, f32[2,2,264,128]{3,2,1,0:T(8,128)}, u32[]{:S(2)}, u32[]{:S(2)}) %collective-permute-start.7) | collective-permute-done | bytes 540704 | tf_op jit(solution)/shard_map/ppermute | solution.py:607
  56.6 0.4 collective-permute-start.8
  57.0 0.1 pad_add_fusion.refs_0_.who_ref
  57.0 0.1 collective-permute-start.3
  57.1 0.0 collective-permute-done.refs_2_
  57.2 0.4 collective-permute-start.6
  57.5 0.0 copy-start.1
  57.5 5.5 %shard_map.103 = (f32[4,2,264,128]{3,2,1,0:T(8,128)S(1)}, f32[2,264,128]{2,1,0:T(8,128)S(1)}, f32[2,264,128]{2,1,0:T(8,128)S(1)}, f32[2,264,128]{2,1,0:T(8,128)S(1)}) custom-call(f32[16,2,24,128]{3,2,1,0:T(8,128)S(1)} %all-to-all-done.refs_0_, bf16[128,768]{1,0:T(8,128)(2,1)} %get-tuple-element.42.refs_1_, ...), custom_call_target="tpu_custom_call", output_to_operand_aliasing={{0}: (3, {})} | custom-call | flops 4000000000 | bytes 2000000 | tf_op jit(solution)/shard_map/pallas_call | solution.py:602
  63.1 0.0 collective-permute-done.3.refs_5_
  63.1 0.0 copy-start.4
  63.1 0.2 collective-permute-start.9
  63.3 0.0 collective-permute-done.6.refs_8_
  63.3 0.8 collective-permute-start.10
  64.1 0.0 collective-permute-done.5.refs_7_
  64.1 0.0 copy-start.2
  64.1 0.2 collective-permute-start.11
  64.3 0.0 collective-permute-done.2.refs_4_
  64.3 0.0 collective-permute-done.8.refs_10_
  64.3 0.0 copy-done.4
  64.4 0.0 copy-done.5
  64.4 0.6 copy-done.2
  65.0 0.2 copy-done.3
  65.1 0.0 copy-done.1
  65.1 0.0 copy-start
  65.1 5.1 %early.1.early_ref = f32[32,256,256]{2,1,0:T(8,128)S(1)} custom-call(s32[2]{0:T(128)S(1)} %pad_add_fusion.refs_0_.who_ref, f32[4,2,264,128]{3,2,1,0:T(8,128)S(1)} %get-tuple-element.25.refs_1_.rest_0_, f32[2,264,128]{2,1,0:T(8,128)} %collective-permute-done.refs_2_, f32[2,2,264,128]{3,2,1,0:T(8,128)} %collective-permute-done.1.refs_3_, ...), custom_call_target="tpu_custom_call" | custom-call | flops 4000000000 | bytes 2000000 | tf_op jit(solution)/shard_map/early/pallas_call | solution.py:633
  70.2 0.0 collective-permute-done.9.rest_1_
  70.3 0.0 collective-permute-done.10.rest_2_
  70.3 2.1 %collective-permute-done.11.rest_3_ = f32[2,264,128]{2,1,0:T(8,128)S(1)} collective-permute-done((f32[2,264,128]{2,1,0:T(8,128)S(1)}, f32[2,264,128]{2,1,0:T(8,128)S(1)}, u32[]{:S(2)}, u32[]{:S(2)}) %collective-permute-start.11) | collective-permute-done | bytes 270368 | tf_op jit(solution)/shard_map/ppermute | solution.py:609
  72.4 0.0 copy-done
  72.4 10.2 %image.1 = f32[256,4096]{1,0:T(8,128)} custom-call(s32[2]{0:T(128)S(1)} %pad_add_fusion.refs_0_.who_ref, f32[32,256,256]{2,1,0:T(8,128)S(1)} %early.1.early_ref, f32[4,2,264,128]{3,2,1,0:T(8,128)S(1)} %get-tuple-element.25.refs_1_.rest_0_, f32[2,264,128]{2,1,0:T(8,128)S(1)} %collective-permute-done.9.rest_1_, ...), custom_call_target="tpu_custom_call" | custom-call | tf_op jit(solution)/shard_map/image/pallas_call | solution.py:639
  (2 shorter events, 0.0 us)
Async XLA Ops:
  3.0 17.3 %all-to-all-start.1 = ((f32[16,2,24,128]{3,2,1,0:T(8,128)}), f32[16,2,24,128]{3,2,1,0:T(8,128)S(1)}, u32[]{:S(2)}, u32[]{:S(2)}) async-start(f32[16,2,24,128]{3,2,1,0:T(8,128)} %get-tuple-element.21), calls=%async_computation.1 | async-start | bytes 786432 | tf_op jit(solution)/shard_map/all_to_all | solution.py:550
  20.3 16.4 %all-to-all-start = ((f32[16,2,24,128]{3,2,1,0:T(8,128)}), f32[16,2,24,128]{3,2,1,0:T(8,128)S(1)}, u32[]{:S(2)}, u32[]{:S(2)}) async-start(f32[16,2,24,128]{3,2,1,0:T(8,128)} %get-tuple-element.20), calls=%async_computation | async-start | bytes 786432 | tf_op jit(solution)/shard_map/all_to_all | solution.py:550
  36.3 13.1 %collective-permute-start.4 = (f32[2,2,264,128]{3,2,1,0:T(8,128)S(1)}, f32[2,2,264,128]{3,2,1,0:T(8,128)}, u32[]{:S(2)}, u32[]{:S(2)}) collective-permute-start(f32[2,2,264,128]{3,2,1,0:T(8,128)S(1)} %get-tuple-element.29), channel_id=1, source_target_pairs={{0,4},{1,3},{2,6},{3,1},{4,0},{5,7},{6,2},{7,5},{8,12},{9,11},{10,... | collective-permute-start | bytes 1622024 | tf_op jit(solution)/shard_map/ppermute | solution.py:607
  36.6 15.4 %collective-permute-start.1 = (f32[2,2,264,128]{3,2,1,0:T(8,128)S(1)}, f32[2,2,264,128]{3,2,1,0:T(8,128)}, u32[]{:S(2)}, u32[]{:S(2)}) collective-permute-start(f32[2,2,264,128]{3,2,1,0:T(8,128)S(1)} %get-tuple-element.27), channel_id=1, source_target_pairs={{0,2},{1,5},{2,0},{3,7},{4,6},{5,1},{6,4},{7,3},{8,10},{9,13},{10,... | collective-permute-start | bytes 1622024 | tf_op jit(solution)/shard_map/ppermute | solution.py:607
  42.3 14.3 %collective-permute-start.7 = (f32[2,2,264,128]{3,2,1,0:T(8,128)S(1)}, f32[2,2,264,128]{3,2,1,0:T(8,128)}, u32[]{:S(2)}, u32[]{:S(2)}) collective-permute-start(f32[2,2,264,128]{3,2,1,0:T(8,128)S(1)} %get-tuple-element.31), channel_id=1, source_target_pairs={{0,2},{1,5},{2,0},{3,7},{4,6},{5,1},{6,4},{7,3},{8,10},{9,13},{10,... | collective-permute-start | bytes 1622024 | tf_op jit(solution)/shard_map/ppermute | solution.py:607
  43.7 13.4 %collective-permute-start = (f32[2,264,128]{2,1,0:T(8,128)S(1)}, f32[2,264,128]{2,1,0:T(8,128)}, u32[]{:S(2)}, u32[]{:S(2)}) collective-permute-start(f32[2,264,128]{2,1,0:T(8,128)S(1)} %get-tuple-element.26), channel_id=1, source_target_pairs={{0,1},{1,0},{2,3},{3,2},{4,5},{5,4},{6,7},{7,6},{8,9},{9,8},{10,11... | collective-permute-start | bytes 811016 | tf_op jit(solution)/shard_map/ppermute | solution.py:612
  49.4 14.8 %collective-permute-start.5 = (f32[2,2,264,128]{3,2,1,0:T(8,128)}, f32[2,2,264,128]{3,2,1,0:T(8,128)S(1)}, u32[]{:S(2)}, u32[]{:S(2)}) collective-permute-start(f32[2,2,264,128]{3,2,1,0:T(8,128)} %collective-permute-done.4.refs_6_), channel_id=1, source_target_pairs={{0,1},{1,0},{2,3},{3,2},{4,5},{5,4},{6,7},{7,6},{8,9},{9,8},{10,11... | collective-permute-start | bytes 1622024 | tf_op jit(solution)/shard_map/ppermute | solution.py:611
  52.0 12.3 %collective-permute-start.2 = (f32[2,2,264,128]{3,2,1,0:T(8,128)}, f32[2,2,264,128]{3,2,1,0:T(8,128)S(1)}, u32[]{:S(2)}, u32[]{:S(2)}) collective-permute-start(f32[2,2,264,128]{3,2,1,0:T(8,128)} %collective-permute-done.1.refs_3_), channel_id=1, source_target_pairs={{0,1},{1,0},{2,3},{3,2},{4,5},{5,4},{6,7},{7,6},{8,9},{9,8},{10,11... | collective-permute-start | bytes 1622024 | tf_op jit(solution)/shard_map/ppermute | solution.py:611
  56.6 7.8 %collective-permute-start.8 = (f32[2,2,264,128]{3,2,1,0:T(8,128)}, f32[2,2,264,128]{3,2,1,0:T(8,128)}, u32[]{:S(2)}, u32[]{:S(2)}) collective-permute-start(f32[2,2,264,128]{3,2,1,0:T(8,128)} %collective-permute-done.7.refs_9_), channel_id=1, source_target_pairs={{0,1},{1,0},{2,3},{3,2},{4,5},{5,4},{6,7},{7,6},{8,9},{9,8},{10,11... | collective-permute-start | bytes 1622024 | tf_op jit(solution)/shard_map/ppermute | solution.py:611
  57.0 6.1 %collective-permute-start.3 = (f32[2,264,128]{2,1,0:T(8,128)S(1)}, f32[2,264,128]{2,1,0:T(8,128)S(1)}, u32[]{:S(2)}, u32[]{:S(2)}) collective-permute-start(f32[2,264,128]{2,1,0:T(8,128)S(1)} %get-tuple-element.28), channel_id=1, source_target_pairs={{0,1},{1,0},{2,3},{3,2},{4,5},{5,4},{6,7},{7,6},{8,9},{9,8},{10,11... | collective-permute-start | bytes 811016 | tf_op jit(solution)/shard_map/ppermute | solution.py:612
  57.2 6.2 %collective-permute-start.6 = (f32[2,264,128]{2,1,0:T(8,128)S(1)}, f32[2,264,128]{2,1,0:T(8,128)S(1)}, u32[]{:S(2)}, u32[]{:S(2)}) collective-permute-start(f32[2,264,128]{2,1,0:T(8,128)S(1)} %get-tuple-element.30), channel_id=1, source_target_pairs={{0,1},{1,0},{2,3},{3,2},{4,5},{5,4},{6,7},{7,6},{8,9},{9,8},{10,11... | collective-permute-start | bytes 811016 | tf_op jit(solution)/shard_map/ppermute | solution.py:612
  57.5 7.6 %copy-start.1 = (f32[64,128]{1,0:T(8,128)S(1)}, f32[64,128]{1,0:T(8,128)}, u32[]{:S(2)}) copy-start(f32[64,128]{1,0:T(8,128)} %constant.66.clone.refs_11_) | copy-start | bytes 98308
  63.1 1.2 %copy-start.4 = (f32[2,264,128]{2,1,0:T(8,128)}, f32[2,264,128]{2,1,0:T(8,128)S(1)}, u32[]{:S(2)}) copy-start(f32[2,264,128]{2,1,0:T(8,128)S(1)} %collective-permute-done.3.refs_5_) | copy-start | bytes 811012
  63.1 7.1 %collective-permute-start.9 = (f32[2,264,128]{2,1,0:T(8,128)S(1)}, f32[2,264,128]{2,1,0:T(8,128)S(1)}, u32[]{:S(2)}, u32[]{:S(2)}) collective-permute-start(f32[2,264,128]{2,1,0:T(8,128)S(1)} %get-tuple-element.32), channel_id=1, source_target_pairs={{0,1},{1,0},{2,3},{3,2},{4,5},{5,4},{6,7},{7,6},{8,9},{9,8},{10,11... | collective-permute-start | bytes 811016 | tf_op jit(solution)/shard_map/ppermute | solution.py:612
  63.3 1.0 %copy-start.5 = (f32[2,264,128]{2,1,0:T(8,128)}, f32[2,264,128]{2,1,0:T(8,128)S(1)}, u32[]{:S(2)}) copy-start(f32[2,264,128]{2,1,0:T(8,128)S(1)} %collective-permute-done.6.refs_8_) | copy-start | bytes 811012
  63.3 6.9 %collective-permute-start.10 = (f32[2,264,128]{2,1,0:T(8,128)S(1)}, f32[2,264,128]{2,1,0:T(8,128)S(1)}, u32[]{:S(2)}, u32[]{:S(2)}) collective-permute-start(f32[2,264,128]{2,1,0:T(8,128)S(1)} %get-tuple-element.33), channel_id=1, source_target_pairs={{0,4},{1,3},{2,6},{3,1},{4,0},{5,7},{6,2},{7,5},{8,12},{9,11},{10,... | collective-permute-start | bytes 811016 | tf_op jit(solution)/shard_map/ppermute | solution.py:607
  64.1 0.8 copy-start.2
  64.1 8.2 %collective-permute-start.11 = (f32[2,264,128]{2,1,0:T(8,128)S(1)}, f32[2,264,128]{2,1,0:T(8,128)S(1)}, u32[]{:S(2)}, u32[]{:S(2)}) collective-permute-start(f32[2,264,128]{2,1,0:T(8,128)S(1)} %get-tuple-element.34), channel_id=1, source_target_pairs={{0,5},{1,2},{2,7},{3,0},{4,1},{5,6},{6,3},{7,4},{8,13},{9,10},{10,... | collective-permute-start | bytes 811016 | tf_op jit(solution)/shard_map/ppermute | solution.py:609
  64.3 0.8 copy-start.3
  65.1 7.2 %copy-start = (f32[64,128]{1,0:T(8,128)S(1)}, f32[64,128]{1,0:T(8,128)}, u32[]{:S(2)}) copy-start(f32[64,128]{1,0:T(8,128)} %constant.68.clone.rest_5_) | copy-start | bytes 98308

commit v2 on v1

--- a/solution.py
+++ b/solution.py
@@ -390,10 +390,22 @@
 def early_kernel(steps, who_ref, *rest):
     mine_ref, *piece_refs, turn_ref, out_ref, near_ref, landed = rest
     sources = [ref if i % 3 == 0 else ref.at[i % 3 - 1] for i, ref in enumerate(piece_refs)]
-    copies = [pltpu.make_async_copy(ref, near_ref.at[i], landed.at[i]) for i, ref in enumerate(sources)]
-    for copy in copies:
+    chunks = landed.shape[0]
+    length = near_ref.shape[2] // chunks
+    copies = [
+        [
+            pltpu.make_async_copy(
+                ref.at[:, pl.ds(chunk * length, length)],
+                near_ref.at[i, :, pl.ds(chunk * length, length)],
+                landed.at[chunk, i],
+            )
+            for i, ref in enumerate(sources)
+        ]
+        for chunk in range(chunks)
+    ]
+    for copy in sum(copies, []):
         copy.start()
-    piece_refs = [near_ref.at[i] for i in range(len(copies))]
+    piece_refs = [near_ref.at[i] for i in range(len(sources))]
 
     def transform(t, carry):
         values = [(None, None)] * SLABS
@@ -412,9 +424,15 @@
                 out_ref[q, pl.ds(base, STRIP), LANES:] = real * s + imag * c
         return carry
 
-    for copy in copies:
-        copy.wait()
-    lax.fori_loop(0, out_ref.shape[1] // STRIP, transform, 0)
+    strips, per, begin = out_ref.shape[1] // STRIP, COARSE // STRIP, 0
+    for chunk in range(chunks):
+        for copy in copies[chunk]:
+            copy.wait()
+        end = begin
+        while end < strips and (end // per) * STEP + (end % per + 1) * STRIP <= (chunk + 1) * length:
+            end += 1
+        lax.fori_loop(begin, end, transform, 0)
+        begin = end
 
 
 def image_kernel(who_ref, early_ref, *rest):
@@ -624,7 +642,7 @@
         out_specs=pl.BlockSpec(memory_space=pltpu.VMEM),
         scratch_shapes=[
             pltpu.VMEM((3 * len(first_steps), 2, own * STEP, LANES), F32),
-            pltpu.SemaphoreType.DMA((3 * len(first_steps),)),
+            pltpu.SemaphoreType.DMA((3, 3 * len(first_steps))),
         ],
         compiler_params=pltpu.CompilerParams(vmem_limit_bytes=6 * 1024 * 1024),
         cost_estimate=pl.CostEstimate(flops=4_000_000_000, bytes_accessed=2_000_000, transcendentals=0),

time: 84 us -> 84.4 us (level)
  no operation moved by 1% of the time
where the time goes in v2:
time: 84.4 us; the launch traced here: 82.9 us
  Pallas kernels  40.5 us (48%)
  waiting for transfers between devices  20.4 us (24%)
  starting transfers between devices  19.2 us (23%)
  local copies, waits for them, and re-layouts  1.73 us (2%)
  other arithmetic  0.86 us (1%)
    pallas_call x4, Pallas kernels, fast_body(): run(taps[phase], matrices[k % 2], twist, *held)  22.4 us
    all_to_all x2, starting transfers between devices, fast_body(): lax.all_to_all(part, group, split_axis=0, concat_axis=0, tiled=True)  11.4 us
    pallas_call x1, Pallas kernels, fast_body(): pl.pallas_call(image_kernel, out_shape=jax.ShapeDtypeStruct((rows, G), F3...  10.2 us
    all_to_all x2, waiting for transfers between devices, fast_body(): lax.all_to_all(part, group, split_axis=0, concat_axis=0, tiled=True)  9.04 us
    ppermute x4, waiting for transfers between devices, fast_body(): lax.ppermute(straight, inner, pairs_of(lambda z, y, c: beside(z, y, c, 0)))  8.97 us
    pallas_call x1, Pallas kernels, fast_body(): run(who, mine, *[far(kind[k]) for k in first_steps for kind in (siblings,...  4.88 us
    ppermute x3, starting transfers between devices, fast_body(): lax.ppermute(straights[k], inner, pairs_of(lambda z, y, c: (z, y, 1 - c)))  3.03 us
    pallas_call x1, Pallas kernels, fast_body(): pl.pallas_call(pack_kernel, out_shape=[pltpu.HBM((senders, steps // phase...  2.99 us
  transfers between devices with their start and end apart: 14, of which 4 were waited for; matrix products, arithmetic and copies ran while one was open for 2% of the time, Pallas kernels for 33%

profile of v2, /device:TPU:13, one launch (start us, length us, event | category | flops | bytes accessed | tf_op | source)
XLA Modules:
  0.0 82.9 jit_solution(6507071701169738868)
XLA Ops:
  0.0 3.0 %pack.1 = (f32[16,2,24,128]{3,2,1,0:T(8,128)}, f32[16,2,24,128]{3,2,1,0:T(8,128)}) custom-call(f32[1,64,256]{2,1,0:T(8,128)} %weight_ref.1, f32[1,64,256]{2,1,0:T(8,128)} %frac_u_ref.1, f32[1,64,256]{2,1,0:T(8,128)} %frac_v_ref.1, s32[1,64,256]{2,1,0:T(8,128)} %code_ref.1, s32[1,64,64]{2,1,0:T(8,128)} %fill_ref.1), custom_call_target="tpu_custom_call" | custom-call | tf_op jit(solution)/shard_map/pack/pallas_call | solution.py:551
  3.0 6.5 %all-to-all-start.1 = ((f32[16,2,24,128]{3,2,1,0:T(8,128)}), f32[16,2,24,128]{3,2,1,0:T(8,128)S(1)}, u32[]{:S(2)}, u32[]{:S(2)}) async-start(f32[16,2,24,128]{3,2,1,0:T(8,128)} %get-tuple-element.21), calls=%async_computation.1 | async-start | bytes 786432 | tf_op jit(solution)/shard_map/all_to_all | solution.py:568
  9.5 0.9 %dynamic-slice_bitcast_fusion.1 = (bf16[32,768]{1,0:T(8,128)(2,1)S(1)}, bf16[32,768]{1,0:T(8,128)(2,1)S(1)}, bf16[32,768]{1,0:T(8,128)(2,1)S(1)}, bf16[32,768]{1...) fusion(bf16[16,32,768]{2,1,0:T(8,128)(2,1)} %constant.64.clone, s32[]{:T(128)S(6)} %select_n.47, ...), kind=kLoop, calls=%fused_computation.4 | loop fusion | bytes 589848 | tf_op jit(solution)/shard_map/jit(dynamic_index_in_dim)/squeeze | solution.py:574
  10.5 0.8 pad_maximum_fusion.2
  11.3 9.0 %all-to-all-done.1.refs_0_ = f32[16,2,24,128]{3,2,1,0:T(8,128)S(1)} async-done(((f32[16,2,24,128]{3,2,1,0:T(8,128)}), f32[16,2,24,128]{3,2,1,0:T(8,128)S(1)}, u32[]{:S(2)}, u32[]{:S(2)}) %all-to-all-start.1) | async-done | bytes 393248 | tf_op jit(solution)/shard_map/all_to_all | solution.py:568
  20.3 4.9 %all-to-all-start = ((f32[16,2,24,128]{3,2,1,0:T(8,128)}), f32[16,2,24,128]{3,2,1,0:T(8,128)S(1)}, u32[]{:S(2)}, u32[]{:S(2)}) async-start(f32[16,2,24,128]{3,2,1,0:T(8,128)} %get-tuple-element.20), calls=%async_computation | async-start | bytes 786432 | tf_op jit(solution)/shard_map/all_to_all | solution.py:568
  25.2 5.5 %shard_map.100 = (f32[4,2,264,128]{3,2,1,0:T(8,128)S(1)}, f32[2,264,128]{2,1,0:T(8,128)S(1)}, f32[2,2,264,128]{3,2,1,0:T(8,128)S(1)}) custom-call(f32[16,2,24,128]{3,2,1,0:T(8,128)S(1)} %all-to-all-done.1.refs_0_, bf16[128,768]{1,0:T(8,128)(2,1)} %get-tuple-element.41.refs_1_, f32[128,128]{1,0:T(8,128)} %constant.65.clone.refs_2_), custom_call_target="tpu_custom_call" | custom-call | flops 4000000000 | bytes 2000000 | tf_op jit(solution)/shard_map/pallas_call | solution.py:620
  30.7 5.6 %shard_map.101 = (f32[4,2,264,128]{3,2,1,0:T(8,128)S(1)}, f32[2,264,128]{2,1,0:T(8,128)S(1)}, f32[2,2,264,128]{3,2,1,0:T(8,128)S(1)}) custom-call(f32[16,2,24,128]{3,2,1,0:T(8,128)S(1)} %all-to-all-done.1.refs_0_, bf16[128,768]{1,0:T(8,128)(2,1)} %get-tuple-element.42.refs_1_, f32[128,128]{1,0:T(8,128)} %constant.65.clone.refs_2_, ...), custom_call_target="tpu_custom_call", output_to_operand_aliasing={{0}: (3, {})} | custom-call | flops 4000000000 | bytes 2000000 | tf_op jit(solution)/shard_map/pallas_call | solution.py:620
  36.3 0.3 collective-permute-start.4
  36.6 0.1 collective-permute-start.1
  36.7 0.0 all-to-all-done.refs_0_
  36.7 5.6 %shard_map.102 = (f32[4,2,264,128]{3,2,1,0:T(8,128)S(1)}, f32[2,264,128]{2,1,0:T(8,128)S(1)}, f32[2,2,264,128]{3,2,1,0:T(8,128)S(1)}) custom-call(f32[16,2,24,128]{3,2,1,0:T(8,128)S(1)} %all-to-all-done.refs_0_, bf16[128,768]{1,0:T(8,128)(2,1)} %get-tuple-element.41.refs_1_, f32[128,128]{1,0:T(8,128)} %constant.65.clone.refs_2_, ...), custom_call_target="tpu_custom_call", output_to_operand_aliasing={{0}: (3, {})} | custom-call | flops 4000000000 | bytes 2000000 | tf_op jit(solution)/shard_map/pallas_call | solution.py:620
  42.3 1.4 %collective-permute-start.7 = (f32[2,2,264,128]{3,2,1,0:T(8,128)S(1)}, f32[2,2,264,128]{3,2,1,0:T(8,128)}, u32[]{:S(2)}, u32[]{:S(2)}) collective-permute-start(f32[2,2,264,128]{3,2,1,0:T(8,128)S(1)} %get-tuple-element.31), channel_id=1, source_target_pairs={{0,2},{1,5},{2,0},{3,7},{4,6},{5,1},{6,4},{7,3},{8,10},{9,13},{10,... | collective-permute-start | bytes 1622024 | tf_op jit(solution)/shard_map/ppermute | solution.py:625
  43.7 1.2 %collective-permute-start = (f32[2,264,128]{2,1,0:T(8,128)S(1)}, f32[2,264,128]{2,1,0:T(8,128)}, u32[]{:S(2)}, u32[]{:S(2)}) collective-permute-start(f32[2,264,128]{2,1,0:T(8,128)S(1)} %get-tuple-element.26), channel_id=1, source_target_pairs={{0,1},{1,0},{2,3},{3,2},{4,5},{5,4},{6,7},{7,6},{8,9},{9,8},{10,11... | collective-permute-start | bytes 811016 | tf_op jit(solution)/shard_map/ppermute | solution.py:630
  44.9 4.4 %collective-permute-done.4.refs_6_ = f32[2,2,264,128]{3,2,1,0:T(8,128)} collective-permute-done((f32[2,2,264,128]{3,2,1,0:T(8,128)S(1)}, f32[2,2,264,128]{3,2,1,0:T(8,128)}, u32[]{:S(2)}, u32[]{:S(2)}) %collective-permute-start.4) | collective-permute-done | bytes 540704 | tf_op jit(solution)/shard_map/ppermute | solution.py:625
  49.4 2.6 %collective-permute-start.5 = (f32[2,2,264,128]{3,2,1,0:T(8,128)}, f32[2,2,264,128]{3,2,1,0:T(8,128)S(1)}, u32[]{:S(2)}, u32[]{:S(2)}) collective-permute-start(f32[2,2,264,128]{3,2,1,0:T(8,128)} %collective-permute-done.4.refs_6_), channel_id=1, source_target_pairs={{0,1},{1,0},{2,3},{3,2},{4,5},{5,4},{6,7},{7,6},{8,9},{9,8},{10,11... | collective-permute-start | bytes 1622024 | tf_op jit(solution)/shard_map/ppermute | solution.py:629
  52.0 0.0 collective-permute-done.1.refs_3_
  52.0 0.0 collective-permute-start.2
  52.0 4.5 %collective-permute-done.7.refs_9_ = f32[2,2,264,128]{3,2,1,0:T(8,128)} collective-permute-done((f32[2,2,264,128]{3,2,1,0:T(8,128)S(1)}, f32[2,2,264,128]{3,2,1,0:T(8,128)}, u32[]{:S(2)}, u32[]{:S(2)}) %collective-permute-start.7) | collective-permute-done | bytes 540704 | tf_op jit(solution)/shard_map/ppermute | solution.py:625
  56.6 0.4 collective-permute-start.8
  57.0 0.1 pad_add_fusion.refs_0_.who_ref
  57.0 0.1 collective-permute-start.3
  57.1 0.0 collective-permute-done.refs_2_
  57.1 0.4 collective-permute-start.6
  57.5 0.0 copy-start.1
  57.5 5.7 %shard_map.103 = (f32[4,2,264,128]{3,2,1,0:T(8,128)S(1)}, f32[2,264,128]{2,1,0:T(8,128)S(1)}, f32[2,264,128]{2,1,0:T(8,128)S(1)}, f32[2,264,128]{2,1,0:T(8,128)S(1)}) custom-call(f32[16,2,24,128]{3,2,1,0:T(8,128)S(1)} %all-to-all-done.refs_0_, bf16[128,768]{1,0:T(8,128)(2,1)} %get-tuple-element.42.refs_1_, ...), custom_call_target="tpu_custom_call", output_to_operand_aliasing={{0}: (3, {})} | custom-call | flops 4000000000 | bytes 2000000 | tf_op jit(solution)/shard_map/pallas_call | solution.py:620
  63.3 0.0 collective-permute-done.3.refs_5_
  63.3 0.0 copy-start.4
  63.3 0.2 collective-permute-start.9
  63.5 0.0 collective-permute-done.6.refs_8_
  63.5 0.0 copy-start.5
  63.5 0.8 collective-permute-start.10
  64.3 0.0 collective-permute-done.5.refs_7_
  64.3 0.0 copy-start.2
  64.3 0.2 collective-permute-start.11
  64.5 0.0 collective-permute-done.2.refs_4_
  64.5 0.0 collective-permute-done.8.refs_10_
  64.5 0.0 copy-done.4
  64.5 0.0 copy-done.5
  64.5 0.6 copy-done.2
  65.1 0.2 copy-done.3
  65.3 0.0 copy-done.1
  65.3 4.9 %early.1.early_ref = f32[32,256,256]{2,1,0:T(8,128)S(1)} custom-call(s32[2]{0:T(128)S(1)} %pad_add_fusion.refs_0_.who_ref, f32[4,2,264,128]{3,2,1,0:T(8,128)S(1)} %get-tuple-element.25.refs_1_.rest_0_, f32[2,264,128]{2,1,0:T(8,128)} %collective-permute-done.refs_2_, f32[2,2,264,128]{3,2,1,0:T(8,128)} %collective-permute-done.1.refs_3_, ...), custom_call_target="tpu_custom_call" | custom-call | flops 4000000000 | bytes 2000000 | tf_op jit(solution)/shard_map/early/pallas_call | solution.py:651
  70.2 0.0 collective-permute-done.9.rest_1_
  70.2 0.0 collective-permute-done.10.rest_2_
  70.2 2.3 %collective-permute-done.11.rest_3_ = f32[2,264,128]{2,1,0:T(8,128)S(1)} collective-permute-done((f32[2,264,128]{2,1,0:T(8,128)S(1)}, f32[2,264,128]{2,1,0:T(8,128)S(1)}, u32[]{:S(2)}, u32[]{:S(2)}) %collective-permute-start.11) | collective-permute-done | bytes 270368 | tf_op jit(solution)/shard_map/ppermute | solution.py:627
  72.6 0.0 copy-done
  72.6 10.2 %image.1 = f32[256,4096]{1,0:T(8,128)} custom-call(s32[2]{0:T(128)S(1)} %pad_add_fusion.refs_0_.who_ref, f32[32,256,256]{2,1,0:T(8,128)S(1)} %early.1.early_ref, f32[4,2,264,128]{3,2,1,0:T(8,128)S(1)} %get-tuple-element.25.refs_1_.rest_0_, f32[2,264,128]{2,1,0:T(8,128)S(1)} %collective-permute-done.9.rest_1_, ...), custom_call_target="tpu_custom_call" | custom-call | tf_op jit(solution)/shard_map/image/pallas_call | solution.py:657
  (2 shorter events, 0.0 us)
Async XLA Ops:
  3.0 17.3 %all-to-all-start.1 = ((f32[16,2,24,128]{3,2,1,0:T(8,128)}), f32[16,2,24,128]{3,2,1,0:T(8,128)S(1)}, u32[]{:S(2)}, u32[]{:S(2)}) async-start(f32[16,2,24,128]{3,2,1,0:T(8,128)} %get-tuple-element.21), calls=%async_computation.1 | async-start | bytes 786432 | tf_op jit(solution)/shard_map/all_to_all | solution.py:568
  20.3 16.4 %all-to-all-start = ((f32[16,2,24,128]{3,2,1,0:T(8,128)}), f32[16,2,24,128]{3,2,1,0:T(8,128)S(1)}, u32[]{:S(2)}, u32[]{:S(2)}) async-start(f32[16,2,24,128]{3,2,1,0:T(8,128)} %get-tuple-element.20), calls=%async_computation | async-start | bytes 786432 | tf_op jit(solution)/shard_map/all_to_all | solution.py:568
  36.3 13.1 %collective-permute-start.4 = (f32[2,2,264,128]{3,2,1,0:T(8,128)S(1)}, f32[2,2,264,128]{3,2,1,0:T(8,128)}, u32[]{:S(2)}, u32[]{:S(2)}) collective-permute-start(f32[2,2,264,128]{3,2,1,0:T(8,128)S(1)} %get-tuple-element.29), channel_id=1, source_target_pairs={{0,4},{1,3},{2,6},{3,1},{4,0},{5,7},{6,2},{7,5},{8,12},{9,11},{10,... | collective-permute-start | bytes 1622024 | tf_op jit(solution)/shard_map/ppermute | solution.py:625
  36.6 15.4 %collective-permute-start.1 = (f32[2,2,264,128]{3,2,1,0:T(8,128)S(1)}, f32[2,2,264,128]{3,2,1,0:T(8,128)}, u32[]{:S(2)}, u32[]{:S(2)}) collective-permute-start(f32[2,2,264,128]{3,2,1,0:T(8,128)S(1)} %get-tuple-element.27), channel_id=1, source_target_pairs={{0,2},{1,5},{2,0},{3,7},{4,6},{5,1},{6,4},{7,3},{8,10},{9,13},{10,... | collective-permute-start | bytes 1622024 | tf_op jit(solution)/shard_map/ppermute | solution.py:625
  42.3 14.3 %collective-permute-start.7 = (f32[2,2,264,128]{3,2,1,0:T(8,128)S(1)}, f32[2,2,264,128]{3,2,1,0:T(8,128)}, u32[]{:S(2)}, u32[]{:S(2)}) collective-permute-start(f32[2,2,264,128]{3,2,1,0:T(8,128)S(1)} %get-tuple-element.31), channel_id=1, source_target_pairs={{0,2},{1,5},{2,0},{3,7},{4,6},{5,1},{6,4},{7,3},{8,10},{9,13},{10,... | collective-permute-start | bytes 1622024 | tf_op jit(solution)/shard_map/ppermute | solution.py:625
  43.7 13.4 %collective-permute-start = (f32[2,264,128]{2,1,0:T(8,128)S(1)}, f32[2,264,128]{2,1,0:T(8,128)}, u32[]{:S(2)}, u32[]{:S(2)}) collective-permute-start(f32[2,264,128]{2,1,0:T(8,128)S(1)} %get-tuple-element.26), channel_id=1, source_target_pairs={{0,1},{1,0},{2,3},{3,2},{4,5},{5,4},{6,7},{7,6},{8,9},{9,8},{10,11... | collective-permute-start | bytes 811016 | tf_op jit(solution)/shard_map/ppermute | solution.py:630
  49.4 14.9 %collective-permute-start.5 = (f32[2,2,264,128]{3,2,1,0:T(8,128)}, f32[2,2,264,128]{3,2,1,0:T(8,128)S(1)}, u32[]{:S(2)}, u32[]{:S(2)}) collective-permute-start(f32[2,2,264,128]{3,2,1,0:T(8,128)} %collective-permute-done.4.refs_6_), channel_id=1, source_target_pairs={{0,1},{1,0},{2,3},{3,2},{4,5},{5,4},{6,7},{7,6},{8,9},{9,8},{10,11... | collective-permute-start | bytes 1622024 | tf_op jit(solution)/shard_map/ppermute | solution.py:629
  52.0 12.5 %collective-permute-start.2 = (f32[2,2,264,128]{3,2,1,0:T(8,128)}, f32[2,2,264,128]{3,2,1,0:T(8,128)S(1)}, u32[]{:S(2)}, u32[]{:S(2)}) collective-permute-start(f32[2,2,264,128]{3,2,1,0:T(8,128)} %collective-permute-done.1.refs_3_), channel_id=1, source_target_pairs={{0,1},{1,0},{2,3},{3,2},{4,5},{5,4},{6,7},{7,6},{8,9},{9,8},{10,11... | collective-permute-start | bytes 1622024 | tf_op jit(solution)/shard_map/ppermute | solution.py:629
  56.6 7.9 %collective-permute-start.8 = (f32[2,2,264,128]{3,2,1,0:T(8,128)}, f32[2,2,264,128]{3,2,1,0:T(8,128)}, u32[]{:S(2)}, u32[]{:S(2)}) collective-permute-start(f32[2,2,264,128]{3,2,1,0:T(8,128)} %collective-permute-done.7.refs_9_), channel_id=1, source_target_pairs={{0,1},{1,0},{2,3},{3,2},{4,5},{5,4},{6,7},{7,6},{8,9},{9,8},{10,11... | collective-permute-start | bytes 1622024 | tf_op jit(solution)/shard_map/ppermute | solution.py:629
  57.0 6.3 %collective-permute-start.3 = (f32[2,264,128]{2,1,0:T(8,128)S(1)}, f32[2,264,128]{2,1,0:T(8,128)S(1)}, u32[]{:S(2)}, u32[]{:S(2)}) collective-permute-start(f32[2,264,128]{2,1,0:T(8,128)S(1)} %get-tuple-element.28), channel_id=1, source_target_pairs={{0,1},{1,0},{2,3},{3,2},{4,5},{5,4},{6,7},{7,6},{8,9},{9,8},{10,11... | collective-permute-start | bytes 811016 | tf_op jit(solution)/shard_map/ppermute | solution.py:630
  57.1 6.3 %collective-permute-start.6 = (f32[2,264,128]{2,1,0:T(8,128)S(1)}, f32[2,264,128]{2,1,0:T(8,128)S(1)}, u32[]{:S(2)}, u32[]{:S(2)}) collective-permute-start(f32[2,264,128]{2,1,0:T(8,128)S(1)} %get-tuple-element.30), channel_id=1, source_target_pairs={{0,1},{1,0},{2,3},{3,2},{4,5},{5,4},{6,7},{7,6},{8,9},{9,8},{10,11... | collective-permute-start | bytes 811016 | tf_op jit(solution)/shard_map/ppermute | solution.py:630
  57.5 7.8 %copy-start.1 = (f32[64,128]{1,0:T(8,128)S(1)}, f32[64,128]{1,0:T(8,128)}, u32[]{:S(2)}) copy-start(f32[64,128]{1,0:T(8,128)} %constant.66.clone.refs_11_) | copy-start | bytes 98308
  63.3 1.2 %copy-start.4 = (f32[2,264,128]{2,1,0:T(8,128)}, f32[2,264,128]{2,1,0:T(8,128)S(1)}, u32[]{:S(2)}) copy-start(f32[2,264,128]{2,1,0:T(8,128)S(1)} %collective-permute-done.3.refs_5_) | copy-start | bytes 811012
  63.3 6.9 %collective-permute-start.9 = (f32[2,264,128]{2,1,0:T(8,128)S(1)}, f32[2,264,128]{2,1,0:T(8,128)S(1)}, u32[]{:S(2)}, u32[]{:S(2)}) collective-permute-start(f32[2,264,128]{2,1,0:T(8,128)S(1)} %get-tuple-element.32), channel_id=1, source_target_pairs={{0,1},{1,0},{2,3},{3,2},{4,5},{5,4},{6,7},{7,6},{8,9},{9,8},{10,11... | collective-permute-start | bytes 811016 | tf_op jit(solution)/shard_map/ppermute | solution.py:630
  63.5 1.0 %copy-start.5 = (f32[2,264,128]{2,1,0:T(8,128)}, f32[2,264,128]{2,1,0:T(8,128)S(1)}, u32[]{:S(2)}) copy-start(f32[2,264,128]{2,1,0:T(8,128)S(1)} %collective-permute-done.6.refs_8_) | copy-start | bytes 811012
  63.5 6.7 %collective-permute-start.10 = (f32[2,264,128]{2,1,0:T(8,128)S(1)}, f32[2,264,128]{2,1,0:T(8,128)S(1)}, u32[]{:S(2)}, u32[]{:S(2)}) collective-permute-start(f32[2,264,128]{2,1,0:T(8,128)S(1)} %get-tuple-element.33), channel_id=1, source_target_pairs={{0,4},{1,3},{2,6},{3,1},{4,0},{5,7},{6,2},{7,5},{8,12},{9,11},{10,... | collective-permute-start | bytes 811016 | tf_op jit(solution)/shard_map/ppermute | solution.py:625
  64.3 0.8 copy-start.2
  64.3 8.2 %collective-permute-start.11 = (f32[2,264,128]{2,1,0:T(8,128)S(1)}, f32[2,264,128]{2,1,0:T(8,128)S(1)}, u32[]{:S(2)}, u32[]{:S(2)}) collective-permute-start(f32[2,264,128]{2,1,0:T(8,128)S(1)} %get-tuple-element.34), channel_id=1, source_target_pairs={{0,5},{1,2},{2,7},{3,0},{4,1},{5,6},{6,3},{7,4},{8,13},{9,10},{10,... | collective-permute-start | bytes 811016 | tf_op jit(solution)/shard_map/ppermute | solution.py:627
  64.5 0.8 copy-start.3
  65.3 7.2 %copy-start = (f32[64,128]{1,0:T(8,128)S(1)}, f32[64,128]{1,0:T(8,128)}, u32[]{:S(2)}) copy-start(f32[64,128]{1,0:T(8,128)} %constant.68.clone.rest_5_) | copy-start | bytes 98308
